TPU v7x, 512 devices: a whole 4x8x8 slice. The times are simulated.
512 devices in a mesh: rows: 8 (over y), tp: 16 (over z, core), copy: 4 (over x).
Axes of the slice: x: 4, y: 8, z: 8, core: 2. Of those that a mesh axis runs over, the one named last changes fastest.
Arguments:
- train_query: float32 [20480, 5120], P(('copy', 'rows'), 'tp'), parts along dimension 0, may hold values from -0.125 to 0.125
- drift_query: float32 [20480, 5120], P(('copy', 'rows'), 'tp'), parts along dimension 0, may hold values from -6 to 6
- spread_query: float32 [20480, 5120], P(('copy', 'rows'), 'tp'), parts along dimension 0, may hold values from 0.1 to 10
- train_key: float32 [20480, 1024], P(('copy', 'rows'), 'tp'), parts along dimension 0, may hold values from -0.125 to 0.125
- drift_key: float32 [20480, 1024], P(('copy', 'rows'), 'tp'), parts along dimension 0, may hold values from -6 to 6
- spread_key: float32 [20480, 1024], P(('copy', 'rows'), 'tp'), parts along dimension 0, may hold values from 0.1 to 10
- train_value: float32 [20480, 1024], P(('copy', 'rows'), 'tp'), parts along dimension 0, may hold values from -0.125 to 0.125
- drift_value: float32 [20480, 1024], P(('copy', 'rows'), 'tp'), parts along dimension 0, may hold values from -6 to 6
- spread_value: float32 [20480, 1024], P(('copy', 'rows'), 'tp'), parts along dimension 0, may hold values from 0.1 to 10
- norm_train: float32 [20480], P(('copy', 'rows', 'tp')), parts along dimension 0, may hold values from 0.25 to 1.75
- norm_step: float32 [20480], P(('copy', 'rows', 'tp')), parts along dimension 0, may hold values from -0.3 to 0.3
Outputs:
- serving_query: bfloat16 [20480, 5120], P('copy', 'tp'), parts along dimension 0
- serving_key: bfloat16 [20480, 1024], P('copy', 'tp'), parts along dimension 0
- serving_value: bfloat16 [20480, 1024], P('copy', 'tp'), parts along dimension 0
- column_query: float32 [20480], P(('copy', 'tp')), parts along dimension 0
- column_key: float32 [4096], P(('copy', 'tp')), parts along dimension 0
- column_value: float32 [4096], P(('copy', 'tp')), parts along dimension 0
- serve_norm: bfloat16 [20480], P('copy'), parts along dimension 0
- whole_query: float32 [20480, 5120], P(('copy', 'rows'), 'tp'), parts along dimension 0
- whole_key: float32 [20480, 1024], P(('copy', 'rows'), 'tp'), parts along dimension 0
- whole_value: float32 [20480, 1024], P(('copy', 'rows'), 'tp'), parts along dimension 0
There are 4 independent parts, one for each index of `copy`. A program takes and returns all parts, laid end to end along the dimension named above; each array names one. Nothing has to cross between parts.
All inputs are finite; a program needn't handle non-finite values. Where the computation divides by a largest or mean magnitude, that divisor is 1e-20 or more.
Results may differ from a plain program's by a relative error of at most 0.001.
Values may be sent and summed in bfloat16 or wider, within the bound.
A program may use at most 64 MiB of HBM per device.

v0:
```python
import jax
import jax.numpy as jnp
from jax import lax
from jax.sharding import Mesh
from jax.sharding import PartitionSpec as P

D_MODEL = 5120
TP = ("tp_0", "tp_1")
COPY_ROWS_TP = ("copy", "rows", "tp_0", "tp_1")
COPY_TP = ("copy", "tp_0", "tp_1")


learn_rate = 0.01
decay_rate = 0.1
tiny_value = 1e-08


def copy_for_each(shard, axis):
    copies = jnp.broadcast_to(shard, (lax.axis_size(axis), *shard.shape))
    return lax.all_to_all(copies, axis, split_axis=0, concat_axis=0, tiled=True)


def taken_together(shard, axis):
    return copy_for_each(shard, axis).sum(axis=0)


def together(arrays, axis):
    ravelled, at, outs = (jnp.concatenate([a.reshape(-1) for a in arrays]), 0, [])
    total = taken_together(ravelled, axis)
    for a in arrays:
        outs.append(total[at : at + a.size].reshape(a.shape))
        at += a.size
    return tuple(outs)


def side_by_side(arrays, axis, dim, along):
    ends, at = ([], 0)
    for a in arrays[:-1]:
        at += a.shape[along]
        ends.append(at)
    both = jnp.concatenate(arrays, axis=along)
    return tuple(jnp.split(lax.all_gather(both, axis, axis=dim, tiled=True), ends, axis=along))


def joined_along(blocks, dim):
    lengths = list(blocks.shape[1:])
    lengths[dim] *= blocks.shape[0]
    return jnp.moveaxis(blocks, 0, dim).reshape(lengths)


def gather_axes(shard, axes, dim):
    far, near = axes
    blocks = copy_for_each(copy_for_each(shard, far), near)
    return joined_along(blocks.swapaxes(0, 1).reshape(-1, *shard.shape), dim)


def local(
    train_query,
    drift_query,
    spread_query,
    train_key,
    drift_key,
    spread_key,
    train_value,
    drift_value,
    spread_value,
    norm_train,
    norm_step,
):
    whole_query = train_query - learn_rate * (
        drift_query / (jnp.sqrt(spread_query) + tiny_value) + decay_rate * train_query
    )
    whole_key = train_key - learn_rate * (
        drift_key / (jnp.sqrt(spread_key) + tiny_value) + decay_rate * train_key
    )
    whole_value = train_value - learn_rate * (
        drift_value / (jnp.sqrt(spread_value) + tiny_value) + decay_rate * train_value
    )
    total_query, total_key, total_value = together(
        (
            jnp.sum(jnp.abs(whole_query), axis=0),
            jnp.sum(jnp.abs(whole_key), axis=0),
            jnp.sum(jnp.abs(whole_value), axis=0),
        ),
        "rows",
    )
    column_query = total_query / D_MODEL
    column_key = total_key / D_MODEL
    column_value = total_value / D_MODEL
    narrow_query, narrow_key, narrow_value = (
        (whole_query / column_query).astype(jnp.bfloat16),
        (whole_key / column_key).astype(jnp.bfloat16),
        (whole_value / column_value).astype(jnp.bfloat16),
    )
    serving_query, serving_key, serving_value = side_by_side(
        (narrow_query, narrow_key, narrow_value), "rows", 0, 1
    )
    serve_norm = gather_axes(
        (norm_train + norm_step).astype(jnp.bfloat16), (("rows", "tp_0"), "tp_1"), 0
    )
    return (
        serving_query,
        serving_key,
        serving_value,
        column_query,
        column_key,
        column_value,
        serve_norm,
        whole_query,
        whole_key,
        whole_value,
    )


def solution(mesh):
    torus = Mesh(
        mesh.devices.reshape(mesh.shape["rows"], 8, 2, mesh.shape["copy"]),
        ("rows", "tp_0", "tp_1", "copy"),
    )
    in_specs = (
        P(("copy", "rows"), TP),
        P(("copy", "rows"), TP),
        P(("copy", "rows"), TP),
        P(("copy", "rows"), TP),
        P(("copy", "rows"), TP),
        P(("copy", "rows"), TP),
        P(("copy", "rows"), TP),
        P(("copy", "rows"), TP),
        P(("copy", "rows"), TP),
        P(COPY_ROWS_TP),
        P(COPY_ROWS_TP),
    )
    out_specs = (
        P("copy", TP),
        P("copy", TP),
        P("copy", TP),
        P(COPY_TP),
        P(COPY_TP),
        P(COPY_TP),
        P("copy"),
        P(("copy", "rows"), TP),
        P(("copy", "rows"), TP),
        P(("copy", "rows"), TP),
    )
    return jax.shard_map(local, mesh=torus, in_specs=in_specs, out_specs=out_specs, check_vma=False)
```

profile of v0, /device:TPU:6, one launch (start us, length us, event | category | flops | bytes accessed | tf_op | source)
XLA Modules:
  0.0 99.7 jit_solution(7586584667766105589)
XLA Ops:
  7.2 0.0 copy-start.6
  7.2 0.0 copy-start.7
  7.2 0.0 copy-start.8
  7.2 0.0 copy-start.3
  7.2 0.0 copy-start.4
  7.2 0.0 copy-start.5
  7.2 0.0 all-gather.2.cloned.1.call-start
  7.3 2.3 %abs_reduce_fusion = (f32[320]{0:T(512)S(1)}, f32[640,320]{0,1:T(8,128)S(1)}) fusion(f32[640,320]{0,1:T(8,128)} %param.11, f32[640,320]{0,1:T(8,128)} %param.12, f32[640,320]{0,1:T(8,128)} %param.13), kind=kLoop, calls=%fused_computation.1 | loop fusion | flops 1638080 | bytes 3278080 | tf_op jit(solution)/shard_map/reduce_sum | solution.py:81
  9.6 0.0 copy-done.6
  9.6 0.0 copy-done.7
  9.6 0.0 copy-done.8
  9.6 0.0 copy-done.3
  9.6 0.0 copy-done.4
  9.6 0.0 copy-done.5
  9.7 0.0 copy-start
  9.7 0.3 abs_reduce_fusion.1
  9.9 0.0 copy-start.1
  10.0 0.0 copy-start.2
  10.0 0.1 pad_maximum_fusion.1
  10.1 14.7 %all_to_all.20 = f32[8,1,448]{2,1,0:T(1,128)S(1)} all-to-all(f32[8,1,448]{2,1,0:T(1,128)S(1)} %broadcast_in_dim.12), channel_id=1, replica_groups=mesh['rows'=8,'tp_0'=8,'tp_1'=2,'copy'=4] {'rows'}, dimensions={0} | all-to-all | bytes 28672 | tf_op jit(solution)/shard_map/all_to_all | solution.py:20
  24.8 0.1 slice_multiply_fusion.2
  24.8 0.0 copy-start.10
  24.8 0.0 copy-start.11
  24.8 0.1 divide_convert_fusion.2
  24.9 0.1 divide_convert_fusion.1
  25.0 0.1 divide_convert_fusion
  25.2 0.0 copy-done
  25.2 0.0 copy-start.12
  25.2 0.0 copy-start.13
  25.2 0.9 pad_maximum_fusion
  26.1 0.0 copy-done.1
  26.1 0.0 copy-done.2
  26.1 0.0 copy-done.10
  26.1 0.0 copy-done.11
  26.1 0.0 copy-done.9
  26.1 0.0 all-gather.2.cloned.1.call-update
  26.1 0.0 copy-done.12
  26.1 0.0 copy-done.13
  26.2 23.2 %all_to_all.21 = bf16[64,1,40]{2,1,0:T(2,128)(2,1)S(1)} all-to-all(bf16[64,1,40]{2,1,0:T(2,128)(2,1)S(1)} %broadcast_in_dim.13), channel_id=1, replica_groups=mesh['rows'=8,'tp_0'=8,'tp_1'=2,'copy'=4] {'rows','tp_0'}, dimensions={0} | all-to-all | bytes 10240 | tf_op jit(solution)/shard_map/all_to_all | solution.py:20
  49.4 0.1 copy.27
  49.5 0.1 reshape.31
  49.6 3.7 %all_to_all.22 = bf16[2,2,1280]{2,1,0:T(2,128)(2,1)S(1)} all-to-all(bf16[2,2,1280]{2,1,0:T(2,128)(2,1)S(1)} %reshape.31), channel_id=1, replica_groups=mesh['rows'=8,'tp_0'=8,'tp_1'=2,'copy'=4] {'tp_1'}, dimensions={0} | all-to-all | bytes 20480 | tf_op jit(solution)/shard_map/all_to_all | solution.py:20
  53.3 0.1 reshape.32
  53.4 0.1 copy.28
  53.5 0.7 reshape_reshape.3
  54.2 32.3 %all-gather.2.cloned.1.call-done = bf16[5120,448]{0,1:T(8,128)(2,1)} async-done(((bf16[640,448]{0,1:T(8,128)(2,1)}), bf16[5120,448]{0,1:T(8,128)(2,1)}) %all-gather.2.cloned.1.call-update) | async-done | bytes 4587536 | tf_op jit(solution)/shard_map/all_gather | solution.py:42
  86.6 2.4 %fusion = (bf16[5120,64]{0,1:T(8,128)(2,1)}, bf16[5120,64]{0,1:T(8,128)(2,1)}) fusion(bf16[5120,448]{0,1:T(8,128)(2,1)} %all-gather.2.cloned.1.call-done), kind=kLoop, calls=%fused_computation.15 | loop fusion | bytes 2621440 | tf_op jit(solution)/shard_map/split | solution.py:42
  89.0 3.8 %split.12 = bf16[5120,320]{0,1:T(8,128)(2,1)} slice(bf16[5120,448]{0,1:T(8,128)(2,1)} %all-gather.2.cloned.1.call-done), slice={[0:5120], [0:320]} | slice | bytes 6553600 | tf_op jit(solution)/shard_map/split | solution.py:42
  (8 shorter events, 0.1 us)
Async XLA Ops:
  7.2 2.4 %copy-start.6 = (f32[640,64]{0,1:T(8,128)S(1)}, f32[640,64]{0,1:T(8,128)}, u32[]{:S(2)}) copy-start(f32[640,64]{0,1:T(8,128)} %param.14) | copy-start | bytes 491524
  7.2 2.4 %copy-start.7 = (f32[640,64]{0,1:T(8,128)S(1)}, f32[640,64]{0,1:T(8,128)}, u32[]{:S(2)}) copy-start(f32[640,64]{0,1:T(8,128)} %param.15) | copy-start | bytes 491524
  7.2 2.4 %copy-start.8 = (f32[640,64]{0,1:T(8,128)S(1)}, f32[640,64]{0,1:T(8,128)}, u32[]{:S(2)}) copy-start(f32[640,64]{0,1:T(8,128)} %param.16) | copy-start | bytes 491524
  7.2 2.4 %copy-start.3 = (f32[640,64]{0,1:T(8,128)S(1)}, f32[640,64]{0,1:T(8,128)}, u32[]{:S(2)}) copy-start(f32[640,64]{0,1:T(8,128)} %param.17) | copy-start | bytes 491524
  7.2 2.4 %copy-start.4 = (f32[640,64]{0,1:T(8,128)S(1)}, f32[640,64]{0,1:T(8,128)}, u32[]{:S(2)}) copy-start(f32[640,64]{0,1:T(8,128)} %param.18) | copy-start | bytes 491524
  7.2 2.4 %copy-start.5 = (f32[640,64]{0,1:T(8,128)S(1)}, f32[640,64]{0,1:T(8,128)}, u32[]{:S(2)}) copy-start(f32[640,64]{0,1:T(8,128)} %param.19) | copy-start | bytes 491524
  7.2 79.3 %all-gather.2.cloned.1.call-start = ((), (), s32[]{:S(2)}) async-start(), calls=%async_computation.3 | async-start | bytes 5160960 | tf_op jit(solution)/shard_map/all_gather | solution.py:42
  9.7 15.5 %copy-start = (f32[640,320]{0,1:T(8,128)}, f32[640,320]{0,1:T(8,128)S(1)}, u32[]{:S(2)}) copy-start(f32[640,320]{0,1:T(8,128)S(1)} %get-tuple-element.11) | copy-start | bytes 2457604
  9.9 16.1 %copy-start.1 = (f32[640,64]{0,1:T(8,128)}, f32[640,64]{0,1:T(8,128)S(1)}, u32[]{:S(2)}) copy-start(f32[640,64]{0,1:T(8,128)S(1)} %get-tuple-element.15) | copy-start | bytes 491524
  10.0 16.1 %copy-start.2 = (f32[640,64]{0,1:T(8,128)}, f32[640,64]{0,1:T(8,128)S(1)}, u32[]{:S(2)}) copy-start(f32[640,64]{0,1:T(8,128)S(1)} %get-tuple-element.21) | copy-start | bytes 491524
  24.8 1.2 %copy-start.10 = (f32[64]{0:T(128)}, f32[64]{0:T(128)S(1)}, u32[]{:S(2)}) copy-start(f32[64]{0:T(128)S(1)} %get-tuple-element.18) | copy-start | bytes 772
  24.8 1.2 %copy-start.11 = (f32[64]{0:T(128)}, f32[64]{0:T(128)S(1)}, u32[]{:S(2)}) copy-start(f32[64]{0:T(128)S(1)} %get-tuple-element.19) | copy-start | bytes 772
  24.8 1.2 %copy-start.9 = (f32[320]{0:T(512)}, f32[320]{0:T(512)S(1)}, u32[]{:S(2)}) copy-start(f32[320]{0:T(512)S(1)} %slice_multiply_fusion) | copy-start | bytes 3844
  25.2 0.9 copy-start.12
  25.2 0.9 copy-start.13
Sparse Core Ops, SparseCore 0:
  26.2 60.2 all-gather.1
where the time goes:
time: 101 us; the launch traced here: 99.7 us
  blocking collectives  41.6 us (41%)
  waiting for transfers between devices  32.4 us (32%)
  between operations  14.3 us (14%)
  local copies, waits for them, and re-layouts  7.46 us (7%)
  other arithmetic  3.94 us (4%)
    all_to_all x3, blocking collectives, copy_for_each(): return lax.all_to_all(copies, axis, split_axis=0, concat_axis=0, tiled=True)  41.6 us
    all_gather x1, waiting for transfers between devices, side_by_side(): lax.all_gather(both, axis, axis=dim, tiled=True)  32.3 us
    split x2, local copies, waits for them, and re-layouts, side_by_side(): jnp.split(lax.all_gather(both, axis, axis=dim, tiled=True), ends, axis=al...  6.26 us
    reduce_sum x1, other arithmetic, local(): jnp.sum(jnp.abs(whole_query), axis=0)  2.31 us
  transfers between devices with their start and end apart: 1, of which 1 were waited for; matrix products, arithmetic and copies ran while one was open for 1% of the time, Pallas kernels for 0%

commit v1 on v0

v1 whole, which is shorter than its diff:
```python
import functools

import jax
import jax.numpy as jnp
from jax import lax
from jax.experimental import pallas as pl
from jax.experimental.pallas import tpu as pltpu
from jax.sharding import PartitionSpec as P

D_MODEL = 5120
MESH = pl.DeviceIdType.MESH

learn_rate = 0.01
decay_rate = 0.1
tiny_value = 1e-08

CHUNK = 64
PARTS = 4


def kernel(
    n,
    m,
    tq, dq, sq, tk, dk, sk, tv, dv, sv, nt, ns,
    out_q, out_k, out_v, col_q, col_k, col_v, out_n, wq, wk, wv,
    bufs, norm_in, sums, tile_n, got_n, rows_n, flat_n,
    in_sem, norm_sem, sum_send, sum_recv, send, recv, n_send, n_recv, n2_send, n2_recv,
):
    me = lax.axis_index("rows")
    tp = lax.axis_index("tp")
    wide = wq.shape[1]
    serve = {"q": out_q, "k": out_k, "v": out_v}
    whole = {"q": wq, "k": wk, "v": wv}
    sources = {"q": (tq, dq, sq), "k": (tk, dk, sk), "v": (tv, dv, sv)}
    chunks = [(name, at) for name in "qkv" for at in range(0, whole[name].shape[0], CHUNK)]
    count = len(chunks)
    group_of = {"q": 0, "k": wq.shape[0] // 8, "v": (wq.shape[0] + wk.shape[0]) // 8}

    barrier = pltpu.get_barrier_semaphore()
    for d in range(1, n):
        pl.semaphore_signal(barrier, inc=1, device_id={"rows": lax.rem(me + d, n)}, device_id_type=MESH)
    for d in range(1, m):
        pl.semaphore_signal(barrier, inc=1, device_id={"tp": lax.rem(tp + d, m)}, device_id_type=MESH)

    def load(c, i):
        name, at = chunks[c]
        return pltpu.make_async_copy(sources[name][i].at[pl.ds(at, CHUNK), :], bufs.at[c, i], in_sem.at[c, i])

    for c in range(count):
        for i in range(3):
            load(c, i).start()
    norm_loads = [pltpu.make_async_copy(ref, norm_in.at[i], norm_sem.at[i]) for i, ref in enumerate((nt, ns))]
    for copy in norm_loads:
        copy.start()

    lane = lax.broadcasted_iota(jnp.int32, (8, 128), 1)
    sub = lax.broadcasted_iota(jnp.int32, (8, 128), 0)

    total = jnp.zeros((8, 128), jnp.float32)
    for c, (name, at) in enumerate(chunks):
        for i in range(3):
            load(c, i).wait()
        for r in range(0, CHUNK, 8):
            t = bufs[c, 0, r : r + 8, :]
            w = t - learn_rate * (
                bufs[c, 1, r : r + 8, :] / (jnp.sqrt(bufs[c, 2, r : r + 8, :]) + tiny_value) + decay_rate * t
            )
            whole[name][at + r : at + r + 8, :] = w
            part = jnp.sum(jnp.abs(w), axis=1, keepdims=True)
            total = jnp.where(lane == group_of[name] + (at + r) // 8, part, total)
    sums[me] = total

    for copy in norm_loads:
        copy.wait()
    short = nt.shape[1]
    gain = norm_in[0] + norm_in[1]
    padded = jnp.concatenate([gain, jnp.zeros((1, 128 - short), jnp.float32)], axis=1)
    turned = pltpu.roll(jnp.broadcast_to(padded, (8, 128)), lax.rem(tp * short, 128), 1)
    place = sub * 128 + lane - tp * short
    tile_n[...] = jnp.where((place >= 0) & (place < short), turned, 0.0)

    pl.semaphore_wait(barrier, n - 1 + m - 1)

    def sums_to(d):
        return pltpu.make_async_remote_copy(
            src_ref=sums.at[me], dst_ref=sums.at[me], send_sem=sum_send.at[d - 1], recv_sem=sum_recv.at[d - 1],
            device_id={"rows": lax.rem(me + d, n)}, device_id_type=MESH,
        )

    for d in (n // 2, *[x for k in range(n // 2 - 1, 0, -1) for x in (k, n - k)]):
        sums_to(d).start()

    def norm_to(d):
        return pltpu.make_async_remote_copy(
            src_ref=tile_n, dst_ref=got_n.at[d - 1], send_sem=n_send.at[d - 1], recv_sem=n_recv.at[d - 1],
            device_id={"tp": lax.rem(tp + d, m)}, device_id_type=MESH,
        )

    for d in range(1, m):
        norm_to(d).start()

    for d in range(1, n):
        sums_to(d).wait_recv()
    every = sums[0]
    for y in range(1, n):
        every = every + sums[y]
    column = every / D_MODEL
    inverse = 1.0 / column

    ways = (1, n - 1)
    half = count // 2

    def piece(way, step, c):
        name, at = chunks[c]
        size = CHUNK
        if step == n // 2:
            if c == half:
                size = CHUNK // 2
                at = at + way * size
            elif (c < half) != (way == 0):
                return None
        return name, at, size

    def hop(way, step, c):
        name, at, size = piece(way, step, c)
        owner = lax.rem(me + (step - 1) * ways[1 - way], n)
        block = serve[name].at[pl.ds(at, size), pl.ds(pl.multiple_of(owner * wide, 128), wide)]
        return pltpu.make_async_remote_copy(
            src_ref=block, dst_ref=block,
            send_sem=send.at[way, step - 1, c], recv_sem=recv.at[way, step - 1, c],
            device_id={"rows": lax.rem(me + ways[way], n)}, device_id_type=MESH,
        )

    def arrived(way, step, c):
        name, at, size = piece(way, step, c)
        owner = lax.rem(me + step * ways[1 - way], n)
        block = serve[name].at[pl.ds(at, size), pl.ds(pl.multiple_of(owner * wide, 128), wide)]
        return pltpu.make_async_remote_copy(
            src_ref=block, dst_ref=block,
            send_sem=send.at[way, step - 1, c], recv_sem=recv.at[way, step - 1, c],
            device_id={"rows": lax.rem(me + ways[way], n)}, device_id_type=MESH,
        )

    mine = pl.ds(pl.multiple_of(me * wide, 128), wide)
    flat = [jnp.zeros((8, 128), jnp.float32) for _ in range(4)]
    for c, (name, at) in enumerate(chunks):
        for r in range(0, CHUNK, 16):
            both = []
            for h in range(0, 16, 8):
                g = group_of[name] + (at + r + h) // 8
                scale = jnp.broadcast_to(inverse[:, g : g + 1], (8, wide))
                both.append(whole[name][at + r + h : at + r + h + 8, :] * scale)
            serve[name][at + r : at + r + 16, mine] = jnp.concatenate(both, axis=0).astype(jnp.bfloat16)
        for way in range(2):
            hop(way, 1, c).start()

    for g in range(group_of["v"] + wv.shape[0] // 8):
        here = (lane // 8 == g % 16) & (sub == lane % 8)
        flat[g // 16] = jnp.where(here, jnp.broadcast_to(column[:, g : g + 1], (8, 128)), flat[g // 16])
    row = jnp.concatenate([jnp.sum(f, axis=0, keepdims=True) for f in flat], axis=1)
    flat_n_at = 0
    for ref in (col_q, col_k, col_v):
        size = ref.shape[1]
        ref[...] = row[:, flat_n_at : flat_n_at + size]
        flat_n_at += size

    for d in range(1, m):
        norm_to(d).wait_recv()
    block = tile_n[...]
    for d in range(1, m):
        block = block + got_n[d - 1]
    rows_n[me] = block

    def row_to(d):
        return pltpu.make_async_remote_copy(
            src_ref=rows_n.at[me], dst_ref=rows_n.at[me], send_sem=n2_send.at[d - 1], recv_sem=n2_recv.at[d - 1],
            device_id={"rows": lax.rem(me + d, n)}, device_id_type=MESH,
        )

    for step in range(2, n // 2 + 1):
        for c in range(count):
            for way in range(2):
                arrived(way, step - 1, c).wait_recv()
                if piece(way, step, c) is not None:
                    hop(way, step, c).start()
        if step == 2:
            for d in range(1, n):
                row_to(d).start()

    for d in range(1, n):
        row_to(d).wait_recv()
    deep = m * short // 128
    for y in range(n):
        flat_n[y * deep : (y + 1) * deep, :] = rows_n[y, 0:deep, :]
    out_n[...] = flat_n[...].astype(jnp.bfloat16)

    for c in range(count):
        for way in range(2):
            if piece(way, n // 2, c) is not None:
                arrived(way, n // 2, c).wait_recv()
    for step in range(1, n // 2 + 1):
        for c in range(count):
            for way in range(2):
                if piece(way, step, c) is not None:
                    hop(way, step, c).wait_send()
    for d in range(1, n):
        sums_to(d).wait_send()
        row_to(d).wait_send()
    for d in range(1, m):
        norm_to(d).wait_send()


def put_out(*refs):
    held, sem = refs[:-1], refs[-1]
    k = len(held) // 2
    copies = []
    for i, (src, dst) in enumerate(zip(held[:k], held[k:])):
        rows = src.shape[0]
        parts = PARTS if rows % (16 * PARTS) == 0 else 1
        for p in range(parts):
            block = pl.ds(p * (rows // parts), rows // parts)
            copies.append(pltpu.make_async_copy(src.at[block, :], dst.at[block, :], sem.at[i, p]))
    for copy in copies:
        copy.start()
    for copy in copies:
        copy.wait()


def local(n, m, *args):
    arrays = [pltpu.with_memory_space_constraint(a.T, pltpu.HBM) for a in args[:9]]
    norm = [pltpu.with_memory_space_constraint(a.reshape(1, -1), pltpu.HBM) for a in args[9:]]
    q, k, v = (arrays[i].shape[0] for i in (0, 3, 6))
    wide = arrays[0].shape[1]
    count = (q + k + v) // CHUNK
    f32, bf16 = jnp.float32, jnp.bfloat16
    short = norm[0].shape[1]
    length = n * m * short
    shapes = (
        [((size, n * wide), bf16) for size in (q, k, v)]
        + [((1, size), f32) for size in (q, k, v)]
        + [((length // 128, 128), bf16)]
        + [((size, wide), f32) for size in (q, k, v)]
    )
    dma = pltpu.SemaphoreType.DMA
    outs = pl.pallas_call(
        functools.partial(kernel, n, m),
        out_shape=[jax.ShapeDtypeStruct(*s) for s in shapes],
        in_specs=[pl.BlockSpec(memory_space=pltpu.HBM)] * 11,
        out_specs=[pl.BlockSpec(memory_space=pltpu.VMEM)] * len(shapes),
        scratch_shapes=[
            pltpu.VMEM((count, 3, CHUNK, wide), f32),
            pltpu.VMEM((2, 1, short), f32),
            pltpu.VMEM((n, 8, 128), f32),
            pltpu.VMEM((8, 128), f32),
            pltpu.VMEM((m - 1, 8, 128), f32),
            pltpu.VMEM((n, 8, 128), f32),
            pltpu.VMEM((length // 128, 128), f32),
            dma((count, 3)),
            dma((2,)),
            dma((n - 1,)),
            dma((n - 1,)),
            dma((2, n // 2, count)),
            dma((2, n // 2, count)),
            dma((m - 1,)),
            dma((m - 1,)),
            dma((n - 1,)),
            dma((n - 1,)),
        ],
        compiler_params=pltpu.CompilerParams(
            collective_id=0, has_side_effects=True, vmem_limit_bytes=32 * 1024 * 1024
        ),
        name="step_and_gather",
    )(*arrays, *norm)
    outs = pl.pallas_call(
        put_out,
        out_shape=[jax.ShapeDtypeStruct(*s) for s in shapes],
        in_specs=[pl.BlockSpec(memory_space=pltpu.VMEM)] * len(shapes),
        out_specs=[pl.BlockSpec(memory_space=pltpu.HBM)] * len(shapes),
        scratch_shapes=[dma((len(shapes), PARTS))],
        compiler_params=pltpu.CompilerParams(vmem_limit_bytes=8 * 1024 * 1024),
        name="put_out",
    )(*outs)
    serving = [a.T for a in outs[:3]]
    columns = [a.reshape(-1) for a in outs[3:6]]
    whole = [a.T for a in outs[7:]]
    return (*serving, *columns, outs[6].reshape(-1), *whole)


def solution(mesh):
    n, m = mesh.shape["rows"], mesh.shape["tp"]
    trained = P(("copy", "rows"), "tp")
    gains = P(("copy", "rows", "tp"))
    in_specs = (trained,) * 9 + (gains,) * 2
    out_specs = (P("copy", "tp"),) * 3 + (P(("copy", "tp")),) * 3 + (P("copy"),) + (trained,) * 3
    return jax.shard_map(
        functools.partial(local, n, m), mesh=mesh, in_specs=in_specs, out_specs=out_specs, check_vma=False
    )
```

time: 101 us -> 68.2 us (0.68); the launches traced: 99.7 us -> 68.1 us
  Pallas kernels: 0 us -> 66.8 us
  blocking collectives: 41.6 us -> 0 us
  waiting for transfers between devices: 32.4 us -> 0 us
  between operations: 14.3 us -> 0.66 us
  local copies, waits for them, and re-layouts: 7.46 us -> 0 us
  other arithmetic: 3.94 us -> 0.6 us
    pallas_call x0 -> x2, Pallas kernels: none -> 66.8 us  [the longest x1 64 us: local(): pl.pallas_call(functools.partial(kernel, n, m), out_shape=[jax.ShapeDtype...]
    all_to_all x3 -> x0, blocking collectives: 41.6 us -> none  [copy_for_each(): return lax.all_to_all(copies, axis, split_axis=0, concat_axis=0, tiled=True)]
    all_gather x1 -> x0, waiting for transfers between devices: 32.3 us -> none  [side_by_side(): lax.all_gather(both, axis, axis=dim, tiled=True)]
    split x2 -> x0, local copies, waits for them, and re-layouts: 6.26 us -> none  [side_by_side(): jnp.split(lax.all_gather(both, axis, axis=dim, tiled=True), ends, axis=al...]
    reduce_sum x3 -> x0, other arithmetic: 2.62 us -> none  [the longest x1 2.31 us: local(): jnp.sum(jnp.abs(whole_query), axis=0)]
  transfers between devices with their start and end apart: 1 -> 0, of which waited for: 1 -> 0; matrix products, arithmetic and copies ran while one was open for 1% -> 0% of each run, Pallas kernels for 0% -> 0%
where the time goes in v1:
time: 68.2 us; the launch traced here: 68.1 us
  Pallas kernels  66.8 us (98%)
    pallas_call x1, Pallas kernels, local(): pl.pallas_call(functools.partial(kernel, n, m), out_shape=[jax.ShapeDtype...  64 us
    pallas_call x1, Pallas kernels, local(): pl.pallas_call(put_out, out_shape=[jax.ShapeDtypeStruct(*s) for s in shap...  2.83 us

profile of v1, /device:TPU:6, one launch (start us, length us, event | category | flops | bytes accessed | tf_op | source)
XLA Modules:
  0.0 68.1 jit_solution(10443236470783639847)
XLA Ops:
  0.6 64.0 %step_and_gather.1 = (bf16[320,5120]{1,0:T(8,128)(2,1)S(1)}, bf16[64,5120]{1,0:T(8,128)(2,1)S(1)}, bf16[64,5120]{1,0:T(8,128)(2,1)S(1)}, f32[1,320]{1,0:T(1,128)...) custom-call(f32[320,640]{1,0:T(8,128)} %bitcast.20, ...), custom_call_target="tpu_custom_call" | custom-call | tf_op jit(solution)/shard_map/step_and_gather/pallas_call | solution.py:245
  64.6 2.8 %put_out.1 = (bf16[320,5120]{1,0:T(8,128)(2,1)}, bf16[64,5120]{1,0:T(8,128)(2,1)}, bf16[64,5120]{1,0:T(8,128)(2,1)}, f32[1,320]{1,0:T(1,128)S(1)}, f32[1,64]{1,0...) custom-call(bf16[320,5120]{1,0:T(8,128)(2,1)S(1)} %get-tuple-element, ...), custom_call_target="tpu_custom_call" | custom-call | tf_op jit(solution)/shard_map/put_out/pallas_call | solution.py:274
  67.5 0.6 reduce

commit v2 on v1

--- a/solution.py
+++ b/solution.py
@@ -23,8 +23,9 @@
     m,
     tq, dq, sq, tk, dk, sk, tv, dv, sv, nt, ns,
     out_q, out_k, out_v, col_q, col_k, col_v, out_n, wq, wk, wv,
-    bufs, norm_in, sums, tile_n, got_n, rows_n, flat_n,
-    in_sem, norm_sem, sum_send, sum_recv, send, recv, n_send, n_recv, n2_send, n2_recv,
+    bufs, norm_in, sums, tile_n, rows_n, flat_n, flat_16, got_n,
+    in_sem, norm_sem, sum_send, sum_recv, send, recv, ready,
+    tile_send, tile_recv, lead_send, lead_recv, last_send, last_recv,
 ):
     me = lax.axis_index("rows")
     tp = lax.axis_index("tp")
@@ -36,11 +37,19 @@
     count = len(chunks)
     group_of = {"q": 0, "k": wq.shape[0] // 8, "v": (wq.shape[0] + wk.shape[0]) // 8}
 
+    leads = me == 0
     barrier = pltpu.get_barrier_semaphore()
     for d in range(1, n):
-        pl.semaphore_signal(barrier, inc=1, device_id={"rows": lax.rem(me + d, n)}, device_id_type=MESH)
-    for d in range(1, m):
-        pl.semaphore_signal(barrier, inc=1, device_id={"tp": lax.rem(tp + d, m)}, device_id_type=MESH)
+        peer = lax.rem(me + d, n)
+
+        @pl.when(peer != 0)
+        def _():
+            pl.semaphore_signal(barrier, inc=1, device_id={"rows": peer}, device_id_type=MESH)
+
+    @pl.when(leads)
+    def _():
+        for d in range(1, m):
+            pl.semaphore_signal(barrier, inc=1, device_id={"tp": lax.rem(tp + d, m)}, device_id_type=MESH)
 
     def load(c, i):
         name, at = chunks[c]
@@ -79,7 +88,14 @@
     place = sub * 128 + lane - tp * short
     tile_n[...] = jnp.where((place >= 0) & (place < short), turned, 0.0)
 
-    pl.semaphore_wait(barrier, n - 1 + m - 1)
+    @pl.when(jnp.logical_not(leads))
+    def _():
+        pl.semaphore_wait(barrier, n - 1)
+        pl.semaphore_signal(ready, inc=1, device_id={"rows": 0}, device_id_type=MESH)
+
+    @pl.when(leads)
+    def _():
+        pl.semaphore_wait(ready, n - 1)
 
     def sums_to(d):
         return pltpu.make_async_remote_copy(
@@ -90,14 +106,27 @@
     for d in (n // 2, *[x for k in range(n // 2 - 1, 0, -1) for x in (k, n - k)]):
         sums_to(d).start()
 
-    def norm_to(d):
-        return pltpu.make_async_remote_copy(
-            src_ref=tile_n, dst_ref=got_n.at[d - 1], send_sem=n_send.at[d - 1], recv_sem=n_recv.at[d - 1],
+    def tile_to_lead(y):
+        return pltpu.make_async_remote_copy(
+            src_ref=tile_n, dst_ref=rows_n.at[y], send_sem=tile_send, recv_sem=tile_recv.at[y - 1],
+            device_id={"rows": 0}, device_id_type=MESH,
+        )
+
+    def lead_to(d):
+        return pltpu.make_async_remote_copy(
+            src_ref=flat_16, dst_ref=got_n.at[d - 1], send_sem=lead_send.at[d - 1], recv_sem=lead_recv.at[d - 1],
             device_id={"tp": lax.rem(tp + d, m)}, device_id_type=MESH,
         )
 
-    for d in range(1, m):
-        norm_to(d).start()
+    def lead_to_row(d):
+        return pltpu.make_async_remote_copy(
+            src_ref=out_n, dst_ref=out_n, send_sem=last_send.at[d - 1], recv_sem=last_recv,
+            device_id={"rows": lax.rem(me + d, n)}, device_id_type=MESH,
+        )
+
+    @pl.when(jnp.logical_not(leads))
+    def _():
+        tile_to_lead(me).start()
 
     for d in range(1, n):
         sums_to(d).wait_recv()
@@ -164,18 +193,27 @@
         ref[...] = row[:, flat_n_at : flat_n_at + size]
         flat_n_at += size
 
-    for d in range(1, m):
-        norm_to(d).wait_recv()
-    block = tile_n[...]
-    for d in range(1, m):
-        block = block + got_n[d - 1]
-    rows_n[me] = block
-
-    def row_to(d):
-        return pltpu.make_async_remote_copy(
-            src_ref=rows_n.at[me], dst_ref=rows_n.at[me], send_sem=n2_send.at[d - 1], recv_sem=n2_recv.at[d - 1],
-            device_id={"rows": lax.rem(me + d, n)}, device_id_type=MESH,
-        )
+    def gather_rows():
+        for y in range(1, n):
+            tile_to_lead(y).wait_recv()
+        rows_n[0] = tile_n[...]
+        deep = m * short // 128
+        for y in range(n):
+            flat_n[y * deep : (y + 1) * deep, :] = rows_n[y, 0:deep, :]
+        flat_16[...] = flat_n[...].astype(jnp.bfloat16)
+        pl.semaphore_wait(barrier, m - 1)
+        for d in range(1, m):
+            lead_to(d).start()
+
+    def gather_tp():
+        for d in range(1, m):
+            lead_to(d).wait_recv()
+        all_n = flat_16[...].astype(jnp.float32)
+        for d in range(1, m):
+            all_n = all_n + got_n[d - 1].astype(jnp.float32)
+        out_n[...] = all_n.astype(jnp.bfloat16)
+        for d in range(1, n):
+            lead_to_row(d).start()
 
     for step in range(2, n // 2 + 1):
         for c in range(count):
@@ -184,15 +222,9 @@
                 if piece(way, step, c) is not None:
                     hop(way, step, c).start()
         if step == 2:
-            for d in range(1, n):
-                row_to(d).start()
-
-    for d in range(1, n):
-        row_to(d).wait_recv()
-    deep = m * short // 128
-    for y in range(n):
-        flat_n[y * deep : (y + 1) * deep, :] = rows_n[y, 0:deep, :]
-    out_n[...] = flat_n[...].astype(jnp.bfloat16)
+            pl.when(leads)(gather_rows)
+        if step == n // 2 - 1:
+            pl.when(leads)(gather_tp)
 
     for c in range(count):
         for way in range(2):
@@ -205,9 +237,18 @@
                     hop(way, step, c).wait_send()
     for d in range(1, n):
         sums_to(d).wait_send()
-        row_to(d).wait_send()
-    for d in range(1, m):
-        norm_to(d).wait_send()
+
+    @pl.when(leads)
+    def _():
+        for d in range(1, m):
+            lead_to(d).wait_send()
+        for d in range(1, n):
+            lead_to_row(d).wait_send()
+
+    @pl.when(jnp.logical_not(leads))
+    def _():
+        tile_to_lead(me).wait_send()
+        lead_to_row(1).wait_recv()
 
 
 def put_out(*refs):
@@ -215,6 +256,9 @@
     k = len(held) // 2
     copies = []
     for i, (src, dst) in enumerate(zip(held[:k], held[k:])):
+        if len(dst.shape) == 1:
+            copies.append(pltpu.make_async_copy(src.at[0], dst, sem.at[i, 0]))
+            continue
         rows = src.shape[0]
         parts = PARTS if rows % (16 * PARTS) == 0 else 1
         for p in range(parts):
@@ -252,19 +296,23 @@
             pltpu.VMEM((2, 1, short), f32),
             pltpu.VMEM((n, 8, 128), f32),
             pltpu.VMEM((8, 128), f32),
-            pltpu.VMEM((m - 1, 8, 128), f32),
             pltpu.VMEM((n, 8, 128), f32),
             pltpu.VMEM((length // 128, 128), f32),
+            pltpu.VMEM((length // 128, 128), bf16),
+            pltpu.VMEM((m - 1, length // 128, 128), bf16),
             dma((count, 3)),
             dma((2,)),
             dma((n - 1,)),
             dma((n - 1,)),
             dma((2, n // 2, count)),
             dma((2, n // 2, count)),
+            pltpu.SemaphoreType.REGULAR,
+            dma,
+            dma((n - 1,)),
             dma((m - 1,)),
             dma((m - 1,)),
             dma((n - 1,)),
-            dma((n - 1,)),
+            dma,
         ],
         compiler_params=pltpu.CompilerParams(
             collective_id=0, has_side_effects=True, vmem_limit_bytes=32 * 1024 * 1024
@@ -273,7 +321,7 @@
     )(*arrays, *norm)
     outs = pl.pallas_call(
         put_out,
-        out_shape=[jax.ShapeDtypeStruct(*s) for s in shapes],
+        out_shape=[jax.ShapeDtypeStruct(s[1:] if s[0] == 1 else s, t) for s, t in shapes],
         in_specs=[pl.BlockSpec(memory_space=pltpu.VMEM)] * len(shapes),
         out_specs=[pl.BlockSpec(memory_space=pltpu.HBM)] * len(shapes),
         scratch_shapes=[dma((len(shapes), PARTS))],
@@ -281,7 +329,7 @@
         name="put_out",
     )(*outs)
     serving = [a.T for a in outs[:3]]
-    columns = [a.reshape(-1) for a in outs[3:6]]
+    columns = outs[3:6]
     whole = [a.T for a in outs[7:]]
     return (*serving, *columns, outs[6].reshape(-1), *whole)
 

time: 68.2 us -> 62.6 us (0.918)
  Pallas kernels: 66.8 us -> 61.3 us
    pallas_call x1, Pallas kernels: 64 us -> 58.5 us  [local(): pl.pallas_call(functools.partial(kernel, n, m), out_shape=[jax.ShapeDtype...]
where the time goes in v2:
time: 62.6 us; the launch traced here: 62 us
  Pallas kernels  61.3 us (98%)
  between operations  0.65 us (1%)
    pallas_call x1, Pallas kernels, local(): pl.pallas_call(functools.partial(kernel, n, m), out_shape=[jax.ShapeDtype...  58.5 us
    pallas_call x1, Pallas kernels, local(): pl.pallas_call(put_out, out_shape=[jax.ShapeDtypeStruct(s[1:] if s[0] ==...  2.83 us

profile of v2, /device:TPU:6, one launch (start us, length us, event | category | flops | bytes accessed | tf_op | source)
XLA Modules:
  0.0 62.0 jit_solution(18208947556363634670)
XLA Ops:
  0.6 58.5 %step_and_gather.1 = (bf16[320,5120]{1,0:T(8,128)(2,1)S(1)}, bf16[64,5120]{1,0:T(8,128)(2,1)S(1)}, bf16[64,5120]{1,0:T(8,128)(2,1)S(1)}, f32[1,320]{1,0:T(1,128)...) custom-call(f32[320,640]{1,0:T(8,128)} %bitcast.18, ...), custom_call_target="tpu_custom_call" | custom-call | tf_op jit(solution)/shard_map/step_and_gather/pallas_call | solution.py:289
  59.1 2.8 %put_out.1 = (bf16[320,5120]{1,0:T(8,128)(2,1)}, bf16[64,5120]{1,0:T(8,128)(2,1)}, bf16[64,5120]{1,0:T(8,128)(2,1)}, f32[320]{0:T(512)}, f32[64]{0:T(128)}, /*in...) custom-call(bf16[320,5120]{1,0:T(8,128)(2,1)S(1)} %get-tuple-element.30.refs, ...), custom_call_target="tpu_custom_call" | custom-call | tf_op jit(solution)/shard_map/put_out/pallas_call | solution.py:322

commit v3 on v2

--- a/solution.py
+++ b/solution.py
@@ -24,7 +24,7 @@
     tq, dq, sq, tk, dk, sk, tv, dv, sv, nt, ns,
     out_q, out_k, out_v, col_q, col_k, col_v, out_n, wq, wk, wv,
     bufs, norm_in, sums, tile_n, rows_n, flat_n, flat_16, got_n,
-    in_sem, norm_sem, sum_send, sum_recv, send, recv, ready,
+    early, in_sem, norm_sem, sum_send, sum_recv, send, recv, ready, early_send, early_recv,
     tile_send, tile_recv, lead_send, lead_recv, last_send, last_recv,
 ):
     me = lax.axis_index("rows")
@@ -46,11 +46,6 @@
         def _():
             pl.semaphore_signal(barrier, inc=1, device_id={"rows": peer}, device_id_type=MESH)
 
-    @pl.when(leads)
-    def _():
-        for d in range(1, m):
-            pl.semaphore_signal(barrier, inc=1, device_id={"tp": lax.rem(tp + d, m)}, device_id_type=MESH)
-
     def load(c, i):
         name, at = chunks[c]
         return pltpu.make_async_copy(sources[name][i].at[pl.ds(at, CHUNK), :], bufs.at[c, i], in_sem.at[c, i])
@@ -61,6 +56,11 @@
     norm_loads = [pltpu.make_async_copy(ref, norm_in.at[i], norm_sem.at[i]) for i, ref in enumerate((nt, ns))]
     for copy in norm_loads:
         copy.start()
+
+    @pl.when(leads)
+    def _():
+        for d in range(1, m):
+            pl.semaphore_signal(barrier, inc=1, device_id={"tp": lax.rem(tp + d, m)}, device_id_type=MESH)
 
     lane = lax.broadcasted_iota(jnp.int32, (8, 128), 1)
     sub = lax.broadcasted_iota(jnp.int32, (8, 128), 0)
@@ -91,11 +91,14 @@
     @pl.when(jnp.logical_not(leads))
     def _():
         pl.semaphore_wait(barrier, n - 1)
+
+    @pl.when(me == n - 1)
+    def _():
         pl.semaphore_signal(ready, inc=1, device_id={"rows": 0}, device_id_type=MESH)
 
     @pl.when(leads)
     def _():
-        pl.semaphore_wait(ready, n - 1)
+        pl.semaphore_wait(ready, 1)
 
     def sums_to(d):
         return pltpu.make_async_remote_copy(
@@ -105,6 +108,19 @@
 
     for d in (n // 2, *[x for k in range(n // 2 - 1, 0, -1) for x in (k, n - k)]):
         sums_to(d).start()
+
+    ways = (1, n - 1)
+    first, first_at = chunks[0]
+
+    def early_to(way):
+        return pltpu.make_async_remote_copy(
+            src_ref=whole[first].at[pl.ds(first_at, CHUNK), :], dst_ref=early.at[way],
+            send_sem=early_send.at[way], recv_sem=early_recv.at[way],
+            device_id={"rows": lax.rem(me + ways[way], n)}, device_id_type=MESH,
+        )
+
+    for way in range(2):
+        early_to(way).start()
 
     def tile_to_lead(y):
         return pltpu.make_async_remote_copy(
@@ -136,7 +152,6 @@
     column = every / D_MODEL
     inverse = 1.0 / column
 
-    ways = (1, n - 1)
     half = count // 2
 
     def piece(way, step, c):
@@ -170,18 +185,24 @@
             device_id={"rows": lax.rem(me + ways[way], n)}, device_id_type=MESH,
         )
 
-    mine = pl.ds(pl.multiple_of(me * wide, 128), wide)
     flat = [jnp.zeros((8, 128), jnp.float32) for _ in range(4)]
-    for c, (name, at) in enumerate(chunks):
+
+    def serve_piece(c, source, source_at, owner):
+        name, at = chunks[c]
+        place = pl.ds(pl.multiple_of(owner * wide, 128), wide)
         for r in range(0, CHUNK, 16):
             both = []
-            for h in range(0, 16, 8):
-                g = group_of[name] + (at + r + h) // 8
+            for h in range(r, r + 16, 8):
+                g = group_of[name] + (at + h) // 8
                 scale = jnp.broadcast_to(inverse[:, g : g + 1], (8, wide))
-                both.append(whole[name][at + r + h : at + r + h + 8, :] * scale)
-            serve[name][at + r : at + r + 16, mine] = jnp.concatenate(both, axis=0).astype(jnp.bfloat16)
+                both.append(source[source_at + h : source_at + h + 8, :] * scale)
+            serve[name][at + r : at + r + 16, place] = jnp.concatenate(both, axis=0).astype(jnp.bfloat16)
+
+    for c, (name, at) in enumerate(chunks[1:], 1):
+        serve_piece(c, whole[name], at, me)
         for way in range(2):
             hop(way, 1, c).start()
+    serve_piece(0, whole[first], first_at, me)
 
     for g in range(group_of["v"] + wv.shape[0] // 8):
         here = (lane // 8 == g % 16) & (sub == lane % 8)
@@ -208,6 +229,8 @@
     def gather_tp():
         for d in range(1, m):
             lead_to(d).wait_recv()
+        for d in range(1, m):
+            lead_to(d).wait_send()
         all_n = flat_16[...].astype(jnp.float32)
         for d in range(1, m):
             all_n = all_n + got_n[d - 1].astype(jnp.float32)
@@ -215,14 +238,33 @@
         for d in range(1, n):
             lead_to_row(d).start()
 
+    def sent(step, c):
+        for way in range(2):
+            if step == 1 and c == 0:
+                early_to(way).wait_send()
+            elif piece(way, step, c) is not None:
+                hop(way, step, c).wait_send()
+
     for step in range(2, n // 2 + 1):
         for c in range(count):
             for way in range(2):
-                arrived(way, step - 1, c).wait_recv()
+                if step == 2 and c == 0:
+                    early_to(way).wait_recv()
+                    serve_piece(0, early.at[way], 0, lax.rem(me + ways[1 - way], n))
+                else:
+                    arrived(way, step - 1, c).wait_recv()
                 if piece(way, step, c) is not None:
                     hop(way, step, c).start()
+            if step > 2:
+                sent(step - 2, c)
         if step == 2:
+            for d in range(1, n):
+                sums_to(d).wait_send()
             pl.when(leads)(gather_rows)
+
+            @pl.when(jnp.logical_not(leads))
+            def _():
+                tile_to_lead(me).wait_send()
         if step == n // 2 - 1:
             pl.when(leads)(gather_tp)
 
@@ -230,24 +272,17 @@
         for way in range(2):
             if piece(way, n // 2, c) is not None:
                 arrived(way, n // 2, c).wait_recv()
-    for step in range(1, n // 2 + 1):
-        for c in range(count):
-            for way in range(2):
-                if piece(way, step, c) is not None:
-                    hop(way, step, c).wait_send()
-    for d in range(1, n):
-        sums_to(d).wait_send()
+        sent(n // 2 - 1, c)
+    for c in range(count):
+        sent(n // 2, c)
 
     @pl.when(leads)
     def _():
-        for d in range(1, m):
-            lead_to(d).wait_send()
         for d in range(1, n):
             lead_to_row(d).wait_send()
 
     @pl.when(jnp.logical_not(leads))
     def _():
-        tile_to_lead(me).wait_send()
         lead_to_row(1).wait_recv()
 
 
@@ -300,6 +335,7 @@
             pltpu.VMEM((length // 128, 128), f32),
             pltpu.VMEM((length // 128, 128), bf16),
             pltpu.VMEM((m - 1, length // 128, 128), bf16),
+            pltpu.VMEM((2, CHUNK, wide), f32),
             dma((count, 3)),
             dma((2,)),
             dma((n - 1,)),
@@ -307,6 +343,8 @@
             dma((2, n // 2, count)),
             dma((2, n // 2, count)),
             pltpu.SemaphoreType.REGULAR,
+            dma((2,)),
+            dma((2,)),
             dma,
             dma((n - 1,)),
             dma((m - 1,)),

time: 62.6 us -> 60.7 us (0.970)
  the two profiles are of different devices: /device:TPU:6 before, /device:TPU:8 now
where the time goes in v3:
time: 60.7 us; the launch traced here: 60.6 us
  Pallas kernels  59.9 us (99%)
  between operations  0.65 us (1%)
    pallas_call x1, Pallas kernels, local(): pl.pallas_call(functools.partial(kernel, n, m), out_shape=[jax.ShapeDtype...  57.1 us
    pallas_call x1, Pallas kernels, local(): pl.pallas_call(put_out, out_shape=[jax.ShapeDtypeStruct(s[1:] if s[0] ==...  2.83 us

profile of v3, /device:TPU:8, one launch (start us, length us, event | category | flops | bytes accessed | tf_op | source)
XLA Modules:
  0.0 60.6 jit_solution(1838117035613144383)
XLA Ops:
  0.6 57.1 %step_and_gather.1 = (bf16[320,5120]{1,0:T(8,128)(2,1)S(1)}, bf16[64,5120]{1,0:T(8,128)(2,1)S(1)}, bf16[64,5120]{1,0:T(8,128)(2,1)S(1)}, f32[1,320]{1,0:T(1,128)...) custom-call(f32[320,640]{1,0:T(8,128)} %bitcast.18, ...), custom_call_target="tpu_custom_call" | custom-call | tf_op jit(solution)/shard_map/step_and_gather/pallas_call | solution.py:324
  57.7 2.8 %put_out.1 = (bf16[320,5120]{1,0:T(8,128)(2,1)}, bf16[64,5120]{1,0:T(8,128)(2,1)}, bf16[64,5120]{1,0:T(8,128)(2,1)}, f32[320]{0:T(512)}, f32[64]{0:T(128)}, /*in...) custom-call(bf16[320,5120]{1,0:T(8,128)(2,1)S(1)} %get-tuple-element.30.refs, ...), custom_call_target="tpu_custom_call" | custom-call | tf_op jit(solution)/shard_map/put_out/pallas_call | solution.py:360

commit v4 on v3

v4 whole, which is shorter than its diff:
```python
import functools

import jax
import jax.numpy as jnp
from jax import lax
from jax.experimental import pallas as pl
from jax.experimental.pallas import tpu as pltpu
from jax.sharding import PartitionSpec as P

D_MODEL = 5120
MESH = pl.DeviceIdType.MESH

learn_rate = 0.01
decay_rate = 0.1
tiny_value = 1e-08

LOAD = 64
PIECES = (64, 128, 128, 128)


def wait_for(sem, ref):
    pltpu.make_async_copy(ref, ref, sem).wait()


def kernel(
    n,
    m,
    tq, dq, sq, tk, dk, sk, tv, dv, sv, nt, ns,
    serve, whole, col_q, col_k, col_v, out_n,
    bufs, norm_in, sums, tile_n, rows_n, flat_n, flat_16, got_n, early,
    in_sem, norm_sem, sum_send, sum_recv, send, recv, final_recv, ready, early_send, early_recv,
    tile_send, tile_recv, lead_send, lead_recv, last_send, last_recv,
):
    me = lax.axis_index("rows")
    tp = lax.axis_index("tp")
    columns, wide = whole.shape
    loads = []
    for refs in ((tq, dq, sq), (tk, dk, sk), (tv, dv, sv)):
        loads += [(refs, at) for at in range(0, refs[0].shape[0], LOAD)]
    pieces, at = [], 0
    for size in PIECES:
        pieces.append((at, size))
        at += size
    count = len(pieces)
    ways = (1, n - 1)

    lead = n // 2
    leads = me == lead
    barrier = pltpu.get_barrier_semaphore()
    for d in range(1, n):
        peer = lax.rem(me + d, n)

        @pl.when(peer != lead)
        def _():
            pl.semaphore_signal(barrier, inc=1, device_id={"rows": peer}, device_id_type=MESH)

    def place(c, i):
        return pl.ds((c * 3 + i) * LOAD, LOAD)

    for c, (refs, at) in enumerate(loads):
        for i in range(3):
            pltpu.make_async_copy(refs[i].at[pl.ds(at, LOAD), :], bufs.at[place(c, i), :], in_sem.at[c]).start()
    for i, ref in enumerate((nt, ns)):
        pltpu.make_async_copy(ref, norm_in.at[i], norm_sem).start()

    @pl.when(leads)
    def _():
        for d in range(1, m):
            pl.semaphore_signal(barrier, inc=1, device_id={"tp": lax.rem(tp + d, m)}, device_id_type=MESH)

    lane = lax.broadcasted_iota(jnp.int32, (8, 128), 1)
    sub = lax.broadcasted_iota(jnp.int32, (8, 128), 0)

    total = jnp.zeros((8, 128), jnp.float32)
    for c in range(len(loads)):
        wait_for(in_sem.at[c], bufs.at[pl.ds(c * 3 * LOAD, 3 * LOAD), :])
        for r in range(0, LOAD, 8):
            t, d, s = (bufs[(c * 3 + i) * LOAD + r : (c * 3 + i) * LOAD + r + 8, :] for i in range(3))
            w = t - learn_rate * (d / (jnp.sqrt(s) + tiny_value) + decay_rate * t)
            at = c * LOAD + r
            whole[at : at + 8, :] = w
            part = jnp.sum(jnp.abs(w), axis=1, keepdims=True)
            total = jnp.where(lane == at // 8, part, total)
    sums[me] = total

    @pl.when(jnp.logical_not(leads))
    def _():
        pl.semaphore_wait(barrier, n - 1)

    @pl.when(me == lead - 1)
    def _():
        pl.semaphore_signal(ready, inc=1, device_id={"rows": lead}, device_id_type=MESH)

    @pl.when(leads)
    def _():
        pl.semaphore_wait(ready, 1)

    for d in (n // 2, *[x for k in range(n // 2 - 1, 0, -1) for x in (k, n - k)]):
        pltpu.make_async_remote_copy(
            src_ref=sums.at[me], dst_ref=sums.at[me], send_sem=sum_send, recv_sem=sum_recv,
            device_id={"rows": lax.rem(me + d, n)}, device_id_type=MESH,
        ).start()

    def early_to(way):
        return pltpu.make_async_remote_copy(
            src_ref=whole.at[pl.ds(0, PIECES[0]), :], dst_ref=early.at[way],
            send_sem=early_send, recv_sem=early_recv.at[way],
            device_id={"rows": lax.rem(me + ways[way], n)}, device_id_type=MESH,
        )

    for way in range(2):
        early_to(way).start()

    wait_for(norm_sem, norm_in)
    short = nt.shape[1]
    gain = norm_in[0] + norm_in[1]
    padded = jnp.concatenate([gain, jnp.zeros((1, 128 - short), jnp.float32)], axis=1)
    turned = pltpu.roll(jnp.broadcast_to(padded, (8, 128)), lax.rem(tp * short, 128), 1)
    spot = sub * 128 + lane - tp * short
    tile_n[...] = jnp.where((spot >= 0) & (spot < short), turned, 0.0)

    def tile_to_lead():
        return pltpu.make_async_remote_copy(
            src_ref=tile_n, dst_ref=rows_n.at[me], send_sem=tile_send, recv_sem=tile_recv,
            device_id={"rows": lead}, device_id_type=MESH,
        )

    @pl.when(jnp.logical_not(leads))
    def _():
        tile_to_lead().start()

    wait_for(sum_recv, sums.at[pl.ds(0, n - 1)])
    every = sums[0]
    for y in range(1, n):
        every = every + sums[y]
    column = every / D_MODEL
    inverse = 1.0 / column

    def piece(way, step, c):
        at, size = pieces[c]
        if step < n // 2:
            return at, size
        low = max(at, way * columns // 2)
        high = min(at + size, (way + 1) * columns // 2)
        return (low, high - low) if low < high else None

    def hop(way, step, c):
        at, size = piece(way, step, c)
        owner = lax.rem(me + (step - 1) * ways[1 - way], n)
        block = serve.at[pl.ds(at, size), pl.ds(pl.multiple_of(owner * wide, 128), wide)]
        return pltpu.make_async_remote_copy(
            src_ref=block, dst_ref=block, send_sem=send.at[way],
            recv_sem=recv.at[way, step - 1, c] if step < n // 2 else final_recv.at[way],
            device_id={"rows": lax.rem(me + ways[way], n)}, device_id_type=MESH,
        )

    def serve_piece(c, source, owner):
        at, size = pieces[c]
        here = pl.ds(pl.multiple_of(owner * wide, 128), wide)
        for r in range(0, size, 16):
            both = []
            for h in range(r, r + 16, 8):
                g = (at + h) // 8
                scale = jnp.broadcast_to(inverse[:, g : g + 1], (8, wide))
                both.append(source[h : h + 8, :] * scale)
            serve[at + r : at + r + 16, here] = jnp.concatenate(both, axis=0).astype(jnp.bfloat16)

    for c in (*range(1, count), 0):
        serve_piece(c, whole.at[pl.ds(*pieces[c]), :], me)
        if c > 0:
            for way in range(2):
                hop(way, 1, c).start()

    flat = [jnp.zeros((8, 128), jnp.float32) for _ in range(4)]
    for g in range(columns // 8):
        here = (lane // 8 == g % 16) & (sub == lane % 8)
        flat[g // 16] = jnp.where(here, jnp.broadcast_to(column[:, g : g + 1], (8, 128)), flat[g // 16])
    row = jnp.concatenate([jnp.sum(f, axis=0, keepdims=True) for f in flat], axis=1)
    at = 0
    for ref in (col_q, col_k, col_v):
        size = ref.shape[1]
        ref[...] = row[:, at : at + size]
        at += size

    def lead_to_tp(d):
        return pltpu.make_async_remote_copy(
            src_ref=flat_16, dst_ref=got_n.at[d - 1], send_sem=lead_send, recv_sem=lead_recv,
            device_id={"tp": lax.rem(tp + d, m)}, device_id_type=MESH,
        )

    def lead_to_row(d):
        return pltpu.make_async_remote_copy(
            src_ref=out_n, dst_ref=out_n, send_sem=last_send, recv_sem=last_recv,
            device_id={"rows": lax.rem(me + d, n)}, device_id_type=MESH,
        )

    def gather_rows():
        wait_for(tile_recv, rows_n.at[pl.ds(0, n - 1)])
        rows_n[me] = tile_n[...]
        deep = m * short // 128
        for y in range(n):
            flat_n[y * deep : (y + 1) * deep, :] = rows_n[y, 0:deep, :]
        flat_16[...] = flat_n[...].astype(jnp.bfloat16)
        pl.semaphore_wait(barrier, m - 1)
        for d in range(1, m):
            lead_to_tp(d).start()

    def gather_tp():
        wait_for(lead_recv, got_n)
        wait_for(lead_send, got_n)
        all_n = flat_16[...].astype(jnp.float32)
        for d in range(1, m):
            all_n = all_n + got_n[d - 1].astype(jnp.float32)
        out_n[...] = all_n.astype(jnp.bfloat16)
        for d in range(1, n):
            lead_to_row(d).start()

    for step in range(2, n // 2 + 1):
        for c in range(count):
            for way in range(2):
                if step == 2 and c == 0:
                    early_to(way).wait_recv()
                    serve_piece(0, early.at[way], lax.rem(me + ways[1 - way], n))
                else:
                    wait_for(recv.at[way, step - 2, c], serve.at[pl.ds(*pieces[c]), pl.ds(0, wide)])
                if piece(way, step, c) is not None:
                    hop(way, step, c).start()
        if step == 2:
            wait_for(sum_send, sums.at[pl.ds(0, n - 1)])
            wait_for(early_send, early)
            pl.when(leads)(gather_rows)

            @pl.when(jnp.logical_not(leads))
            def _():
                tile_to_lead().wait_send()

        if step == n // 2 - 1:
            pl.when(leads)(gather_tp)

    for way in range(2):
        wait_for(final_recv.at[way], bufs.at[pl.ds(0, columns // 4), :])
    for way in range(2):
        hops = (n // 2 - 1) * columns + columns // 2 - PIECES[0]
        wait_for(send.at[way], bufs.at[pl.ds(0, hops // 2), :])

    @pl.when(leads)
    def _():
        wait_for(last_send, got_n.at[pl.ds(0, n - 1)])

    @pl.when(jnp.logical_not(leads))
    def _():
        wait_for(last_recv, out_n)


def put_out(
    serve, whole, col_q, col_k, col_v, norm,
    out_q, out_k, out_v, out_col_q, out_col_k, out_col_v, out_n, whole_q, whole_k, whole_v,
    sem,
):
    copies = []

    def put(src, dst):
        copies.append(pltpu.make_async_copy(src, dst, sem.at[len(copies)]))
        copies[-1].start()

    for src, dsts in ((serve, (out_q, out_k, out_v)), (whole, (whole_q, whole_k, whole_v))):
        at = 0
        for dst in dsts:
            put(src.at[pl.ds(at, dst.shape[0]), :], dst)
            at += dst.shape[0]
    for src, dst in ((col_q, out_col_q), (col_k, out_col_k), (col_v, out_col_v)):
        put(src.at[0], dst)
    put(norm, out_n)
    for copy in copies:
        copy.wait()


def local(n, m, *args):
    arrays = [pltpu.with_memory_space_constraint(a.T, pltpu.HBM) for a in args[:9]]
    norm = [pltpu.with_memory_space_constraint(a.reshape(1, -1), pltpu.HBM) for a in args[9:]]
    sizes = [arrays[i].shape[0] for i in (0, 3, 6)]
    columns, wide = sum(sizes), arrays[0].shape[1]
    f32, bf16 = jnp.float32, jnp.bfloat16
    length = n * m * norm[0].shape[1]
    flat = (length // 128, 128)
    count = len(PIECES)
    dma, vmem, shape = pltpu.SemaphoreType.DMA, pltpu.VMEM, jax.ShapeDtypeStruct
    held = [
        shape((columns, n * wide), bf16),
        shape((columns, wide), f32),
        *[shape((1, size), f32) for size in sizes],
        shape(flat, bf16),
    ]
    outs = pl.pallas_call(
        functools.partial(kernel, n, m),
        out_shape=held,
        in_specs=[pl.BlockSpec(memory_space=pltpu.HBM)] * 11,
        out_specs=[pl.BlockSpec(memory_space=vmem)] * len(held),
        scratch_shapes=[
            vmem((3 * columns, wide), f32),
            vmem((2, 1, norm[0].shape[1]), f32),
            vmem((n, 8, 128), f32),
            vmem((8, 128), f32),
            vmem((n, 8, 128), f32),
            vmem(flat, f32),
            vmem(flat, bf16),
            vmem((m - 1, *flat), bf16),
            vmem((2, PIECES[0], wide), f32),
            dma((columns // LOAD,)),
            dma,
            dma,
            dma,
            dma((2,)),
            dma((2, n // 2 - 1, count)),
            dma((2,)),
            pltpu.SemaphoreType.REGULAR,
            dma,
            dma((2,)),
            *[dma] * 6,
        ],
        compiler_params=pltpu.CompilerParams(
            collective_id=0, has_side_effects=True, vmem_limit_bytes=32 * 1024 * 1024
        ),
        name="step_and_gather",
    )(*arrays, *norm)
    results = [
        *[shape((size, n * wide), bf16) for size in sizes],
        *[shape((size,), f32) for size in sizes],
        shape(flat, bf16),
        *[shape((size, wide), f32) for size in sizes],
    ]
    outs = pl.pallas_call(
        put_out,
        out_shape=results,
        in_specs=[pl.BlockSpec(memory_space=vmem)] * len(held),
        out_specs=[pl.BlockSpec(memory_space=pltpu.HBM)] * len(results),
        scratch_shapes=[dma((len(results),))],
        compiler_params=pltpu.CompilerParams(vmem_limit_bytes=8 * 1024 * 1024),
        name="put_out",
    )(*outs)
    serving, scales, gain, kept = outs[:3], outs[3:6], outs[6], outs[7:]
    return (*[a.T for a in serving], *scales, gain.reshape(-1), *[a.T for a in kept])


def solution(mesh):
    n, m = mesh.shape["rows"], mesh.shape["tp"]
    trained = P(("copy", "rows"), "tp")
    gains = P(("copy", "rows", "tp"))
    in_specs = (trained,) * 9 + (gains,) * 2
    out_specs = (P("copy", "tp"),) * 3 + (P(("copy", "tp")),) * 3 + (P("copy"),) + (trained,) * 3
    return jax.shard_map(
        functools.partial(local, n, m), mesh=mesh, in_specs=in_specs, out_specs=out_specs, check_vma=False
    )
```

time: 60.7 us -> 58.6 us (0.965)
  the two profiles are of different devices: /device:TPU:8 before, /device:TPU:6 now
where the time goes in v4:
time: 58.6 us; the launch traced here: 57.6 us
  Pallas kernels  56.9 us (97%)
  between operations  0.65 us (1%)
    pallas_call x1, Pallas kernels, local(): pl.pallas_call(functools.partial(kernel, n, m), out_shape=held, in_specs=...  54.3 us
    pallas_call x1, Pallas kernels, local(): pl.pallas_call(put_out, out_shape=results, in_specs=[pl.BlockSpec(memory_...  2.57 us

profile of v4, /device:TPU:6, one launch (start us, length us, event | category | flops | bytes accessed | tf_op | source)
XLA Modules:
  0.0 57.6 jit_solution(14198987362691517603)
XLA Ops:
  0.6 54.3 %step_and_gather.1 = (bf16[448,5120]{1,0:T(8,128)(2,1)S(1)}, f32[448,640]{1,0:T(8,128)S(1)}, f32[1,320]{1,0:T(1,128)S(1)}, f32[1,64]{1,0:T(1,128)S(1)}, f32[1,64...) custom-call(f32[320,640]{1,0:T(8,128)} %bitcast.18, f32[320,640]{1,0:T(8,128)} %bitcast.19, f32[320,640]{1,0:T(8,128)} %bitcast.20, ...), custom_call_target="tpu_custom_call" | custom-call | tf_op jit(solution)/shard_map/step_and_gather/pallas_call | solution.py:294
  55.0 2.6 %put_out.1 = (bf16[320,5120]{1,0:T(8,128)(2,1)}, bf16[64,5120]{1,0:T(8,128)(2,1)}, bf16[64,5120]{1,0:T(8,128)(2,1)}, f32[320]{0:T(512)}, f32[64]{0:T(128)}, /*in...) custom-call(bf16[448,5120]{1,0:T(8,128)(2,1)S(1)} %get-tuple-element.26.serv, ...), custom_call_target="tpu_custom_call" | custom-call | tf_op jit(solution)/shard_map/put_out/pallas_call | solution.py:332

commit v5 on v4

v5 whole, which is shorter than its diff:
```python
import functools

import jax
import jax.numpy as jnp
from jax import lax
from jax.experimental import pallas as pl
from jax.experimental.pallas import tpu as pltpu
from jax.sharding import PartitionSpec as P

D_MODEL = 5120
MESH = pl.DeviceIdType.MESH

learn_rate = 0.01
decay_rate = 0.1
tiny_value = 1e-08

LOAD = 64
PIECE = 64
EARLY = (48, 48, 0, 96)


def pieces_of(columns, first):
    pieces, at = [(0, first)], first
    while at < columns:
        size = min(PIECE, columns - at)
        pieces.append((at, size))
        at += size
    return pieces


def wait_for(sem, ref):
    pltpu.make_async_copy(ref, ref, sem).wait()


def kernel(
    n,
    m,
    tq, dq, sq, tk, dk, sk, tv, dv, sv, nt, ns,
    serve, whole, col_q, col_k, col_v, out_n,
    bufs, norm_in, sums, tile_n, rows_n, flat_n, flat_16, got_n, early,
    in_sem, norm_sem, sum_send, sum_recv, send, recv, final_recv, ready, early_send, early_recv,
    tile_send, tile_recv, lead_send, lead_recv, last_send, last_recv,
):
    me = lax.axis_index("rows")
    tp = lax.axis_index("tp")
    columns, wide = whole.shape
    loads = []
    for refs in ((tq, dq, sq), (tk, dk, sk), (tv, dv, sv)):
        loads += [(refs, at) for at in range(0, refs[0].shape[0], LOAD)]
    ways = (1, n - 1)

    lead = n // 4
    leads = me == lead
    barrier = pltpu.get_barrier_semaphore()
    for d in range(1, n):
        peer = lax.rem(me + d, n)

        @pl.when(peer != lead)
        def _():
            pl.semaphore_signal(barrier, inc=1, device_id={"rows": peer}, device_id_type=MESH)

    def place(c, i):
        return pl.ds((c * 3 + i) * LOAD, LOAD)

    for c, (refs, at) in enumerate(loads):
        for i in range(3):
            pltpu.make_async_copy(refs[i].at[pl.ds(at, LOAD), :], bufs.at[place(c, i), :], in_sem.at[c]).start()
    for i, ref in enumerate((nt, ns)):
        pltpu.make_async_copy(ref, norm_in.at[i], norm_sem).start()

    @pl.when(leads)
    def _():
        for d in range(1, m):
            pl.semaphore_signal(barrier, inc=1, device_id={"tp": lax.rem(tp + d, m)}, device_id_type=MESH)

    lane = lax.broadcasted_iota(jnp.int32, (8, 128), 1)
    sub = lax.broadcasted_iota(jnp.int32, (8, 128), 0)

    total = jnp.zeros((8, 128), jnp.float32)
    for c in range(len(loads)):
        wait_for(in_sem.at[c], bufs.at[pl.ds(c * 3 * LOAD, 3 * LOAD), :])
        for r in range(0, LOAD, 8):
            t, d, s = (bufs[(c * 3 + i) * LOAD + r : (c * 3 + i) * LOAD + r + 8, :] for i in range(3))
            w = t - learn_rate * (d / (jnp.sqrt(s) + tiny_value) + decay_rate * t)
            at = c * LOAD + r
            whole[at : at + 8, :] = w
            part = jnp.sum(jnp.abs(w), axis=1, keepdims=True)
            total = jnp.where(lane == at // 8, part, total)
    sums[me] = total

    @pl.when(jnp.logical_not(leads))
    def _():
        pl.semaphore_wait(barrier, n - 1)

    @pl.when(me == lead + 1)
    def _():
        pl.semaphore_signal(ready, inc=1, device_id={"rows": lead}, device_id_type=MESH)

    @pl.when(leads)
    def _():
        pl.semaphore_wait(ready, 1)

    for d in (n // 2, *[x for k in range(n // 2 - 1, 0, -1) for x in (k, n - k)]):
        pltpu.make_async_remote_copy(
            src_ref=sums.at[me], dst_ref=sums.at[me], send_sem=sum_send, recv_sem=sum_recv,
            device_id={"rows": lax.rem(me + d, n)}, device_id_type=MESH,
        ).start()

    short = nt.shape[1]

    def tile_to_lead():
        return pltpu.make_async_remote_copy(
            src_ref=tile_n, dst_ref=rows_n.at[me], send_sem=tile_send, recv_sem=tile_recv,
            device_id={"rows": lead}, device_id_type=MESH,
        )

    def place_gain():
        wait_for(norm_sem, norm_in)
        gain = norm_in[0] + norm_in[1]
        padded = jnp.concatenate([gain, jnp.zeros((1, 128 - short), jnp.float32)], axis=1)
        turned = pltpu.roll(jnp.broadcast_to(padded, (8, 128)), lax.rem(tp * short, 128), 1)
        spot = sub * 128 + lane - tp * short
        tile_n[...] = jnp.where((spot >= 0) & (spot < short), turned, 0.0)

        @pl.when(jnp.logical_not(leads))
        def _():
            tile_to_lead().start()

    def rest(first):
        pieces = pieces_of(columns, first)
        live = [c for c, (at, size) in enumerate(pieces) if size > 0]

        def early_to(way):
            return pltpu.make_async_remote_copy(
                src_ref=whole.at[pl.ds(0, first), :], dst_ref=early.at[way, pl.ds(0, first), :],
                send_sem=early_send, recv_sem=early_recv.at[way],
                device_id={"rows": lax.rem(me + ways[way], n)}, device_id_type=MESH,
            )

        if first > 0:
            for way in range(2):
                early_to(way).start()
        place_gain()

        wait_for(sum_recv, sums.at[pl.ds(0, n - 1)])
        every = sums[0]
        for y in range(1, n):
            every = every + sums[y]
        column = every / D_MODEL
        inverse = 1.0 / column

        def piece(way, step, c):
            at, size = pieces[c]
            if step < n // 2:
                return at, size
            low = max(at, way * columns // 2)
            high = min(at + size, (way + 1) * columns // 2)
            return (low, high - low) if low < high else None

        def hop(way, step, c):
            at, size = piece(way, step, c)
            owner = lax.rem(me + (step - 1) * ways[1 - way], n)
            block = serve.at[pl.ds(at, size), pl.ds(pl.multiple_of(owner * wide, 128), wide)]
            return pltpu.make_async_remote_copy(
                src_ref=block, dst_ref=block, send_sem=send.at[way],
                recv_sem=recv.at[way, step - 1, c] if step < n // 2 else final_recv.at[way],
                device_id={"rows": lax.rem(me + ways[way], n)}, device_id_type=MESH,
            )

        def serve_piece(c, source, owner):
            at, size = pieces[c]
            here = pl.ds(pl.multiple_of(owner * wide, 128), wide)
            for r in range(0, size, 16):
                both = []
                for h in range(r, r + 16, 8):
                    g = (at + h) // 8
                    scale = jnp.broadcast_to(inverse[:, g : g + 1], (8, wide))
                    both.append(source[h : h + 8, :] * scale)
                serve[at + r : at + r + 16, here] = jnp.concatenate(both, axis=0).astype(jnp.bfloat16)

        for c in (*live[1:], live[0]) if first > 0 else live:
            serve_piece(c, whole.at[pl.ds(*pieces[c]), :], me)
            if c > 0:
                for way in range(2):
                    hop(way, 1, c).start()

        flat = [jnp.zeros((8, 128), jnp.float32) for _ in range(4)]
        for g in range(columns // 8):
            here = (lane // 8 == g % 16) & (sub == lane % 8)
            flat[g // 16] = jnp.where(here, jnp.broadcast_to(column[:, g : g + 1], (8, 128)), flat[g // 16])
        row = jnp.concatenate([jnp.sum(f, axis=0, keepdims=True) for f in flat], axis=1)
        at = 0
        for ref in (col_q, col_k, col_v):
            size = ref.shape[1]
            ref[...] = row[:, at : at + size]
            at += size

        def lead_to_tp(d):
            return pltpu.make_async_remote_copy(
                src_ref=flat_16, dst_ref=got_n.at[d - 1], send_sem=lead_send, recv_sem=lead_recv,
                device_id={"tp": lax.rem(tp + d, m)}, device_id_type=MESH,
            )

        def lead_to_row(d):
            return pltpu.make_async_remote_copy(
                src_ref=out_n, dst_ref=out_n, send_sem=last_send, recv_sem=last_recv,
                device_id={"rows": lax.rem(me + d, n)}, device_id_type=MESH,
            )

        def gather_rows():
            wait_for(tile_recv, rows_n.at[pl.ds(0, n - 1)])
            rows_n[me] = tile_n[...]
            deep = m * short // 128
            for y in range(n):
                flat_n[y * deep : (y + 1) * deep, :] = rows_n[y, 0:deep, :]
            flat_16[...] = flat_n[...].astype(jnp.bfloat16)
            pl.semaphore_wait(barrier, m - 1)
            for d in range(1, m):
                lead_to_tp(d).start()

        def gather_tp():
            wait_for(lead_recv, got_n)
            wait_for(lead_send, got_n)
            all_n = flat_16[...].astype(jnp.float32)
            for d in range(1, m):
                all_n = all_n + got_n[d - 1].astype(jnp.float32)
            out_n[...] = all_n.astype(jnp.bfloat16)
            for d in range(1, n):
                lead_to_row(d).start()

        for step in range(2, n // 2 + 1):
            for c in live:
                for way in range(2):
                    if step == 2 and c == 0:
                        early_to(way).wait_recv()
                        serve_piece(0, early.at[way], lax.rem(me + ways[1 - way], n))
                    else:
                        wait_for(recv.at[way, step - 2, c], serve.at[pl.ds(*pieces[c]), pl.ds(0, wide)])
                    if piece(way, step, c) is not None:
                        hop(way, step, c).start()
            if step == 2:
                wait_for(sum_send, sums.at[pl.ds(0, n - 1)])
                if first > 0:
                    wait_for(early_send, early.at[:, pl.ds(0, first), :])
                pl.when(leads)(gather_rows)

                @pl.when(jnp.logical_not(leads))
                def _():
                    tile_to_lead().wait_send()

            if step == n // 2 - 1:
                pl.when(leads)(gather_tp)

        for way in range(2):
            wait_for(final_recv.at[way], bufs.at[pl.ds(0, columns // 4), :])
        for way in range(2):
            hops = (n // 2 - 1) * columns + columns // 2 - first
            wait_for(send.at[way], bufs.at[pl.ds(0, hops // 2), :])

        @pl.when(leads)
        def _():
            wait_for(last_send, got_n.at[pl.ds(0, n - 1)])

        @pl.when(jnp.logical_not(leads))
        def _():
            wait_for(last_recv, out_n)

    ring0 = (lax.axis_index("copy") == 0) & (tp < 2)
    core = lax.rem(tp, 2)
    for k, first in enumerate(EARLY):
        pl.when((core == k % 2) & (ring0 == (k >= 2)))(functools.partial(rest, first))


def put_out(
    serve, whole, col_q, col_k, col_v, norm,
    out_q, out_k, out_v, out_col_q, out_col_k, out_col_v, out_n, whole_q, whole_k, whole_v,
    sem,
):
    copies = []

    def put(src, dst):
        copies.append(pltpu.make_async_copy(src, dst, sem.at[len(copies)]))
        copies[-1].start()

    for src, dsts in ((serve, (out_q, out_k, out_v)), (whole, (whole_q, whole_k, whole_v))):
        at = 0
        for dst in dsts:
            put(src.at[pl.ds(at, dst.shape[0]), :], dst)
            at += dst.shape[0]
    for src, dst in ((col_q, out_col_q), (col_k, out_col_k), (col_v, out_col_v)):
        put(src.at[0], dst)
    put(norm, out_n)
    for copy in copies:
        copy.wait()


def local(n, m, *args):
    arrays = [pltpu.with_memory_space_constraint(a.T, pltpu.HBM) for a in args[:9]]
    norm = [pltpu.with_memory_space_constraint(a.reshape(1, -1), pltpu.HBM) for a in args[9:]]
    sizes = [arrays[i].shape[0] for i in (0, 3, 6)]
    columns, wide = sum(sizes), arrays[0].shape[1]
    f32, bf16 = jnp.float32, jnp.bfloat16
    length = n * m * norm[0].shape[1]
    flat = (length // 128, 128)
    count = max(len(pieces_of(columns, first)) for first in EARLY)
    dma, vmem, shape = pltpu.SemaphoreType.DMA, pltpu.VMEM, jax.ShapeDtypeStruct
    held = [
        shape((columns, n * wide), bf16),
        shape((columns, wide), f32),
        *[shape((1, size), f32) for size in sizes],
        shape(flat, bf16),
    ]
    outs = pl.pallas_call(
        functools.partial(kernel, n, m),
        out_shape=held,
        in_specs=[pl.BlockSpec(memory_space=pltpu.HBM)] * 11,
        out_specs=[pl.BlockSpec(memory_space=vmem)] * len(held),
        scratch_shapes=[
            vmem((3 * columns, wide), f32),
            vmem((2, 1, norm[0].shape[1]), f32),
            vmem((n, 8, 128), f32),
            vmem((8, 128), f32),
            vmem((n, 8, 128), f32),
            vmem(flat, f32),
            vmem(flat, bf16),
            vmem((m - 1, *flat), bf16),
            vmem((2, max(EARLY), wide), f32),
            dma((columns // LOAD,)),
            dma,
            dma,
            dma,
            dma((2,)),
            dma((2, n // 2 - 1, count)),
            dma((2,)),
            pltpu.SemaphoreType.REGULAR,
            dma,
            dma((2,)),
            *[dma] * 6,
        ],
        compiler_params=pltpu.CompilerParams(
            collective_id=0, has_side_effects=True, vmem_limit_bytes=32 * 1024 * 1024
        ),
        name="step_and_gather",
    )(*arrays, *norm)
    results = [
        *[shape((size, n * wide), bf16) for size in sizes],
        *[shape((size,), f32) for size in sizes],
        shape(flat, bf16),
        *[shape((size, wide), f32) for size in sizes],
    ]
    outs = pl.pallas_call(
        put_out,
        out_shape=results,
        in_specs=[pl.BlockSpec(memory_space=vmem)] * len(held),
        out_specs=[pl.BlockSpec(memory_space=pltpu.HBM)] * len(results),
        scratch_shapes=[dma((len(results),))],
        compiler_params=pltpu.CompilerParams(vmem_limit_bytes=8 * 1024 * 1024),
        name="put_out",
    )(*outs)
    serving, scales, gain, kept = outs[:3], outs[3:6], outs[6], outs[7:]
    return (*[a.T for a in serving], *scales, gain.reshape(-1), *[a.T for a in kept])


def solution(mesh):
    n, m = mesh.shape["rows"], mesh.shape["tp"]
    trained = P(("copy", "rows"), "tp")
    gains = P(("copy", "rows", "tp"))
    in_specs = (trained,) * 9 + (gains,) * 2
    out_specs = (P("copy", "tp"),) * 3 + (P(("copy", "tp")),) * 3 + (P("copy"),) + (trained,) * 3
    return jax.shard_map(
        functools.partial(local, n, m), mesh=mesh, in_specs=in_specs, out_specs=out_specs, check_vma=False
    )
```

time: 58.6 us -> 57.6 us (0.983); the launches traced: 57.6 us -> 57.2 us
  no operation moved by 1% of the time
where the time goes in v5:
time: 57.6 us; the launch traced here: 57.2 us
  Pallas kernels  56.6 us (98%)
  between operations  0.65 us (1%)
    pallas_call x1, Pallas kernels, local(): pl.pallas_call(functools.partial(kernel, n, m), out_shape=held, in_specs=...  54 us
    pallas_call x1, Pallas kernels, local(): pl.pallas_call(put_out, out_shape=results, in_specs=[pl.BlockSpec(memory_...  2.57 us

profile of v5, /device:TPU:6, one launch (start us, length us, event | category | flops | bytes accessed | tf_op | source)
XLA Modules:
  0.0 57.2 jit_solution(6965590853243216939)
XLA Ops:
  0.6 54.0 %step_and_gather.1 = (bf16[448,5120]{1,0:T(8,128)(2,1)S(1)}, f32[448,640]{1,0:T(8,128)S(1)}, f32[1,320]{1,0:T(1,128)S(1)}, f32[1,64]{1,0:T(1,128)S(1)}, f32[1,64...) custom-call(f32[320,640]{1,0:T(8,128)} %bitcast.18, f32[320,640]{1,0:T(8,128)} %bitcast.19, f32[320,640]{1,0:T(8,128)} %bitcast.20, ...), custom_call_target="tpu_custom_call" | custom-call | tf_op jit(solution)/shard_map/step_and_gather/pallas_call | solution.py:313
  54.7 2.6 %put_out.1 = (bf16[320,5120]{1,0:T(8,128)(2,1)}, bf16[64,5120]{1,0:T(8,128)(2,1)}, bf16[64,5120]{1,0:T(8,128)(2,1)}, f32[320]{0:T(512)}, f32[64]{0:T(128)}, /*in...) custom-call(bf16[448,5120]{1,0:T(8,128)(2,1)S(1)} %get-tuple-element.26.serv, ...), custom_call_target="tpu_custom_call" | custom-call | tf_op jit(solution)/shard_map/put_out/pallas_call | solution.py:351

commit v6 on v5

--- a/solution.py
+++ b/solution.py
@@ -15,17 +15,29 @@
 tiny_value = 1e-08
 
 LOAD = 64
-PIECE = 64
-EARLY = (48, 48, 0, 96)
-
-
-def pieces_of(columns, first):
-    pieces, at = [(0, first)], first
-    while at < columns:
-        size = min(PIECE, columns - at)
-        pieces.append((at, size))
-        at += size
-    return pieces
+GROUPS = (2, 2, 2, 1)
+PIECES = ((64, 128, 128, 128), (48, 144, 128, 128), (0, 128, 128, 128, 64), (96, 96, 128, 128))
+
+
+def pieces_of(sizes):
+    return [(sum(sizes[:c]), size) for c, size in enumerate(sizes)]
+
+
+def last_part(columns, way, at, size):
+    low = max(at, way * columns // 2)
+    high = min(at + size, (way + 1) * columns // 2)
+    return (low, high - low) if low < high else None
+
+
+def slots_of(n, columns, sizes):
+    slots = []
+    for c, (at, size) in enumerate(pieces_of(sizes)):
+        for way in range(2):
+            for step in range(1, n // 2):
+                on = step < n // 2 - 1 or last_part(columns, way, at, size) is not None
+                if size > 0 and on and (step, c) != (1, 0):
+                    slots.append((way, step, c))
+    return slots
 
 
 def wait_for(sem, ref):
@@ -62,9 +74,10 @@
     def place(c, i):
         return pl.ds((c * 3 + i) * LOAD, LOAD)
 
+    group = [g for g, size in enumerate(GROUPS) for _ in range(size)]
     for c, (refs, at) in enumerate(loads):
         for i in range(3):
-            pltpu.make_async_copy(refs[i].at[pl.ds(at, LOAD), :], bufs.at[place(c, i), :], in_sem.at[c]).start()
+            pltpu.make_async_copy(refs[i].at[pl.ds(at, LOAD), :], bufs.at[place(c, i), :], in_sem.at[group[c]]).start()
     for i, ref in enumerate((nt, ns)):
         pltpu.make_async_copy(ref, norm_in.at[i], norm_sem).start()
 
@@ -78,7 +91,8 @@
 
     total = jnp.zeros((8, 128), jnp.float32)
     for c in range(len(loads)):
-        wait_for(in_sem.at[c], bufs.at[pl.ds(c * 3 * LOAD, 3 * LOAD), :])
+        if c == 0 or group[c] != group[c - 1]:
+            wait_for(in_sem.at[group[c]], bufs.at[pl.ds(c * 3 * LOAD, GROUPS[group[c]] * 3 * LOAD), :])
         for r in range(0, LOAD, 8):
             t, d, s = (bufs[(c * 3 + i) * LOAD + r : (c * 3 + i) * LOAD + r + 8, :] for i in range(3))
             w = t - learn_rate * (d / (jnp.sqrt(s) + tiny_value) + decay_rate * t)
@@ -126,8 +140,8 @@
         def _():
             tile_to_lead().start()
 
-    def rest(first):
-        pieces = pieces_of(columns, first)
+    def rest(sizes):
+        pieces, first = pieces_of(sizes), sizes[0]
         live = [c for c, (at, size) in enumerate(pieces) if size > 0]
 
         def early_to(way):
@@ -149,13 +163,14 @@
         column = every / D_MODEL
         inverse = 1.0 / column
 
+        slots = slots_of(n, columns, sizes)
+
         def piece(way, step, c):
-            at, size = pieces[c]
-            if step < n // 2:
-                return at, size
-            low = max(at, way * columns // 2)
-            high = min(at + size, (way + 1) * columns // 2)
-            return (low, high - low) if low < high else None
+            return pieces[c] if step < n // 2 else last_part(columns, way, *pieces[c])
+
+        def arrival(way, step, c):
+            key = (way, step, c)
+            return recv.at[slots.index(key)] if key in slots else final_recv.at[way]
 
         def hop(way, step, c):
             at, size = piece(way, step, c)
@@ -163,7 +178,7 @@
             block = serve.at[pl.ds(at, size), pl.ds(pl.multiple_of(owner * wide, 128), wide)]
             return pltpu.make_async_remote_copy(
                 src_ref=block, dst_ref=block, send_sem=send.at[way],
-                recv_sem=recv.at[way, step - 1, c] if step < n // 2 else final_recv.at[way],
+                recv_sem=arrival(way, step, c),
                 device_id={"rows": lax.rem(me + ways[way], n)}, device_id_type=MESH,
             )
 
@@ -178,11 +193,20 @@
                     both.append(source[h : h + 8, :] * scale)
                 serve[at + r : at + r + 16, here] = jnp.concatenate(both, axis=0).astype(jnp.bfloat16)
 
-        for c in (*live[1:], live[0]) if first > 0 else live:
-            serve_piece(c, whole.at[pl.ds(*pieces[c]), :], me)
-            if c > 0:
-                for way in range(2):
-                    hop(way, 1, c).start()
+        ahead = live[:1] if first > 0 else []
+        orders = [ahead + live[len(ahead) :], ahead + live[len(ahead) :][::-1]]
+        done, put = [], [len(ahead)] * 2
+        for pair in zip(*(order[len(ahead) :] for order in orders)):
+            for c in pair:
+                if c not in done:
+                    serve_piece(c, whole.at[pl.ds(*pieces[c]), :], me)
+                    done.append(c)
+            for way, order in enumerate(orders):
+                while put[way] < len(order) and order[put[way]] in done:
+                    hop(way, 1, order[put[way]]).start()
+                    put[way] += 1
+        if first > 0:
+            serve_piece(0, whole.at[pl.ds(0, first), :], me)
 
         flat = [jnp.zeros((8, 128), jnp.float32) for _ in range(4)]
         for g in range(columns // 8):
@@ -229,13 +253,13 @@
                 lead_to_row(d).start()
 
         for step in range(2, n // 2 + 1):
-            for c in live:
-                for way in range(2):
+            for pair in zip(*orders):
+                for way, c in enumerate(pair):
                     if step == 2 and c == 0:
                         early_to(way).wait_recv()
                         serve_piece(0, early.at[way], lax.rem(me + ways[1 - way], n))
-                    else:
-                        wait_for(recv.at[way, step - 2, c], serve.at[pl.ds(*pieces[c]), pl.ds(0, wide)])
+                    elif (way, step - 1, c) in slots:
+                        wait_for(arrival(way, step - 1, c), serve.at[pl.ds(*pieces[c]), pl.ds(0, wide)])
                     if piece(way, step, c) is not None:
                         hop(way, step, c).start()
             if step == 2:
@@ -252,7 +276,10 @@
                 pl.when(leads)(gather_tp)
 
         for way in range(2):
-            wait_for(final_recv.at[way], bufs.at[pl.ds(0, columns // 4), :])
+            last = columns // 2
+            for c in live:
+                last += pieces[c][1] if (way, n // 2 - 1, c) not in slots else 0
+            wait_for(final_recv.at[way], bufs.at[pl.ds(0, last // 2), :])
         for way in range(2):
             hops = (n // 2 - 1) * columns + columns // 2 - first
             wait_for(send.at[way], bufs.at[pl.ds(0, hops // 2), :])
@@ -267,8 +294,8 @@
 
     ring0 = (lax.axis_index("copy") == 0) & (tp < 2)
     core = lax.rem(tp, 2)
-    for k, first in enumerate(EARLY):
-        pl.when((core == k % 2) & (ring0 == (k >= 2)))(functools.partial(rest, first))
+    for k, sizes in enumerate(PIECES):
+        pl.when((core == k % 2) & (ring0 == (k >= 2)))(functools.partial(rest, sizes))
 
 
 def put_out(
@@ -276,22 +303,19 @@
     out_q, out_k, out_v, out_col_q, out_col_k, out_col_v, out_n, whole_q, whole_k, whole_v,
     sem,
 ):
-    copies = []
-
-    def put(src, dst):
-        copies.append(pltpu.make_async_copy(src, dst, sem.at[len(copies)]))
-        copies[-1].start()
-
-    for src, dsts in ((serve, (out_q, out_k, out_v)), (whole, (whole_q, whole_k, whole_v))):
+    for k, (src, dsts) in enumerate(((serve, (out_q, out_k, out_v)), (whole, (whole_q, whole_k, whole_v)))):
         at = 0
         for dst in dsts:
-            put(src.at[pl.ds(at, dst.shape[0]), :], dst)
+            pltpu.make_async_copy(src.at[pl.ds(at, dst.shape[0]), :], dst, sem.at[k]).start()
             at += dst.shape[0]
-    for src, dst in ((col_q, out_col_q), (col_k, out_col_k), (col_v, out_col_v)):
-        put(src.at[0], dst)
-    put(norm, out_n)
+    small = ((col_q.at[0], out_col_q), (col_k.at[0], out_col_k), (col_v.at[0], out_col_v), (norm, out_n))
+    copies = [pltpu.make_async_copy(*pair, sem.at[2 + k]) for k, pair in enumerate(small)]
+    for copy in copies:
+        copy.start()
     for copy in copies:
         copy.wait()
+    for k, src in enumerate((serve, whole)):
+        wait_for(sem.at[k], src)
 
 
 def local(n, m, *args):
@@ -302,7 +326,7 @@
     f32, bf16 = jnp.float32, jnp.bfloat16
     length = n * m * norm[0].shape[1]
     flat = (length // 128, 128)
-    count = max(len(pieces_of(columns, first)) for first in EARLY)
+    count = max(len(slots_of(n, columns, pieces)) for pieces in PIECES)
     dma, vmem, shape = pltpu.SemaphoreType.DMA, pltpu.VMEM, jax.ShapeDtypeStruct
     held = [
         shape((columns, n * wide), bf16),
@@ -324,13 +348,13 @@
             vmem(flat, f32),
             vmem(flat, bf16),
             vmem((m - 1, *flat), bf16),
-            vmem((2, max(EARLY), wide), f32),
-            dma((columns // LOAD,)),
+            vmem((2, max(pieces[0] for pieces in PIECES), wide), f32),
+            dma((len(GROUPS),)),
             dma,
             dma,
             dma,
             dma((2,)),
-            dma((2, n // 2 - 1, count)),
+            dma((count,)),
             dma((2,)),
             pltpu.SemaphoreType.REGULAR,
             dma,
@@ -353,7 +377,7 @@
         out_shape=results,
         in_specs=[pl.BlockSpec(memory_space=vmem)] * len(held),
         out_specs=[pl.BlockSpec(memory_space=pltpu.HBM)] * len(results),
-        scratch_shapes=[dma((len(results),))],
+        scratch_shapes=[dma((6,))],
         compiler_params=pltpu.CompilerParams(vmem_limit_bytes=8 * 1024 * 1024),
         name="put_out",
     )(*outs)

time: 57.6 us -> 57.1 us (level)
  no operation moved by 1% of the time
where the time goes in v6:
time: 57.1 us; the launch traced here: 56.9 us
  Pallas kernels  56.3 us (99%)
  between operations  0.65 us (1%)
    pallas_call x1, Pallas kernels, local(): pl.pallas_call(functools.partial(kernel, n, m), out_shape=held, in_specs=...  53.7 us
    pallas_call x1, Pallas kernels, local(): pl.pallas_call(put_out, out_shape=results, in_specs=[pl.BlockSpec(memory_...  2.53 us

profile of v6, /device:TPU:6, one launch (start us, length us, event | category | flops | bytes accessed | tf_op | source)
XLA Modules:
  0.0 56.9 jit_solution(15945720518302902460)
XLA Ops:
  0.6 53.7 %step_and_gather.1 = (bf16[448,5120]{1,0:T(8,128)(2,1)S(1)}, f32[448,640]{1,0:T(8,128)S(1)}, f32[1,320]{1,0:T(1,128)S(1)}, f32[1,64]{1,0:T(1,128)S(1)}, f32[1,64...) custom-call(f32[320,640]{1,0:T(8,128)} %bitcast.18, f32[320,640]{1,0:T(8,128)} %bitcast.19, f32[320,640]{1,0:T(8,128)} %bitcast.20, ...), custom_call_target="tpu_custom_call" | custom-call | tf_op jit(solution)/shard_map/step_and_gather/pallas_call | solution.py:337
  54.4 2.5 %put_out.1 = (bf16[320,5120]{1,0:T(8,128)(2,1)}, bf16[64,5120]{1,0:T(8,128)(2,1)}, bf16[64,5120]{1,0:T(8,128)(2,1)}, f32[320]{0:T(512)}, f32[64]{0:T(128)}, /*in...) custom-call(bf16[448,5120]{1,0:T(8,128)(2,1)S(1)} %get-tuple-element.26.serv, ...), custom_call_target="tpu_custom_call" | custom-call | tf_op jit(solution)/shard_map/put_out/pallas_call | solution.py:375

commit v7 on v6

--- a/solution.py
+++ b/solution.py
@@ -71,13 +71,13 @@
         def _():
             pl.semaphore_signal(barrier, inc=1, device_id={"rows": peer}, device_id_type=MESH)
 
-    def place(c, i):
-        return pl.ds((c * 3 + i) * LOAD, LOAD)
-
     group = [g for g, size in enumerate(GROUPS) for _ in range(size)]
     for c, (refs, at) in enumerate(loads):
         for i in range(3):
-            pltpu.make_async_copy(refs[i].at[pl.ds(at, LOAD), :], bufs.at[place(c, i), :], in_sem.at[group[c]]).start()
+            for half in range(0, LOAD, LOAD // 2):
+                source = refs[i].at[pl.ds(at + half, LOAD // 2), :]
+                here = bufs.at[pl.ds((c * 3 + i) * LOAD + half, LOAD // 2), :]
+                pltpu.make_async_copy(source, here, in_sem.at[group[c]]).start()
     for i, ref in enumerate((nt, ns)):
         pltpu.make_async_copy(ref, norm_in.at[i], norm_sem).start()
 
@@ -306,7 +306,10 @@
     for k, (src, dsts) in enumerate(((serve, (out_q, out_k, out_v)), (whole, (whole_q, whole_k, whole_v)))):
         at = 0
         for dst in dsts:
-            pltpu.make_async_copy(src.at[pl.ds(at, dst.shape[0]), :], dst, sem.at[k]).start()
+            size = max(dst.shape[0] // 4, 32)
+            for part in range(0, dst.shape[0], size):
+                here, there = pl.ds(at + part, size), pl.ds(part, size)
+                pltpu.make_async_copy(src.at[here, :], dst.at[there, :], sem.at[k]).start()
             at += dst.shape[0]
     small = ((col_q.at[0], out_col_q), (col_k.at[0], out_col_k), (col_v.at[0], out_col_v), (norm, out_n))
     copies = [pltpu.make_async_copy(*pair, sem.at[2 + k]) for k, pair in enumerate(small)]

time: 57.1 us -> 57.1 us (level)
  no operation moved by 1% of the time
where the time goes in v7:
time: 57.1 us; the launch traced here: 56.9 us
  Pallas kernels  56.2 us (98%)
  between operations  0.65 us (1%)
    pallas_call x1, Pallas kernels, local(): pl.pallas_call(functools.partial(kernel, n, m), out_shape=held, in_specs=...  53.7 us
    pallas_call x1, Pallas kernels, local(): pl.pallas_call(put_out, out_shape=results, in_specs=[pl.BlockSpec(memory_...  2.51 us

profile of v7, /device:TPU:6, one launch (start us, length us, event | category | flops | bytes accessed | tf_op | source)
XLA Modules:
  0.0 56.9 jit_solution(7741925311871421508)
XLA Ops:
  0.6 53.7 %step_and_gather.1 = (bf16[448,5120]{1,0:T(8,128)(2,1)S(1)}, f32[448,640]{1,0:T(8,128)S(1)}, f32[1,320]{1,0:T(1,128)S(1)}, f32[1,64]{1,0:T(1,128)S(1)}, f32[1,64...) custom-call(f32[320,640]{1,0:T(8,128)} %bitcast.18, f32[320,640]{1,0:T(8,128)} %bitcast.19, f32[320,640]{1,0:T(8,128)} %bitcast.20, ...), custom_call_target="tpu_custom_call" | custom-call | tf_op jit(solution)/shard_map/step_and_gather/pallas_call | solution.py:340
  54.4 2.5 %put_out.1 = (bf16[320,5120]{1,0:T(8,128)(2,1)}, bf16[64,5120]{1,0:T(8,128)(2,1)}, bf16[64,5120]{1,0:T(8,128)(2,1)}, f32[320]{0:T(512)}, f32[64]{0:T(128)}, /*in...) custom-call(bf16[448,5120]{1,0:T(8,128)(2,1)S(1)} %get-tuple-element.26.serv, ...), custom_call_target="tpu_custom_call" | custom-call | tf_op jit(solution)/shard_map/put_out/pallas_call | solution.py:378
